TPU v7x, 256 devices: a whole 4x4x8 slice. The times are simulated.
256 devices in a mesh: tower: 16 (over z, x_hi), dev: 16 (over x_lo, y, core).
Axes of the slice: x: 4 (x_hi: 2, x_lo: 2; x = x_hi * 2 + x_lo), y: 4, z: 8, core: 2. Of those that a mesh axis runs over, the one named last changes fastest.
Arguments:
- ids: int32 [16, 16, 2048, 32], P('tower', 'dev'), may hold values from 0 to 511
- tables: bfloat16 [16, 16, 512, 128], P('tower', 'dev'), may hold values from -1 to 1
- order: int32 [2048], replicated, may hold values from 0 to 2047, each once
- w_first: bfloat16 [16, 2048, 1024], P('tower', 'dev'), may hold values from -0.125 to 0.125
- w_second: bfloat16 [16, 1024, 512], P('tower'), may hold values from -0.1875 to 0.1875
- w_head: bfloat16 [8192, 128], replicated, may hold values from -0.0625 to 0.0625
- w_interact: float32 [256, 128], replicated, may hold values from -0.1875 to 0.1875
Outputs:
- scores: float32 [16, 128, 128], P('dev', 'tower')
Inputs may be any that keep to these rules, and one draw needn't show every extreme that they name: order is a permutation of the batch rows 0 to 2047.
All inputs are finite; a program needn't handle non-finite values.
Results may differ from a plain program's by a relative error of at most 0.0023.
Values may be sent and summed in bfloat16 or wider, within the bound.
A program may use at most 64 MiB of HBM per device.

v0:
```python
import math

import jax
import jax.numpy as jnp
from jax import lax
from jax.sharding import PartitionSpec as P


def pool_feature(feature_ids, table):
    samples = feature_ids.shape[0]
    active = table.shape[0]
    block = math.gcd(samples, 512)
    blocked = feature_ids.reshape(samples // block, block, feature_ids.shape[1])
    positions = lax.broadcasted_iota(jnp.int32, (1, 1, active), 2)

    def pool_block(block_ids):
        tally = jnp.sum((block_ids[:, :, None] == positions).astype(jnp.int32), axis=1)
        return jnp.dot(
            tally.astype(jnp.bfloat16), table, preferred_element_type=jnp.float32
        ).astype(jnp.bfloat16)

    pooled = lax.map(pool_block, blocked)
    return pooled.reshape(samples, table.shape[1])


def on_device(ids, tables, order, w_first, w_second, w_head, w_interact):
    towers = lax.axis_size("tower")
    devices = lax.axis_size("dev")
    samples = ids.shape[2]
    my_rows = samples // devices
    pieces = pool_feature(ids[0, 0], tables[0, 0])
    features = jnp.take(pieces, order, axis=0)
    received = lax.all_to_all(features, "dev", split_axis=0, concat_axis=1, tiled=True)
    preact = jnp.dot(
        received,
        lax.all_gather(w_first[0], "dev", axis=0, tiled=True),
        preferred_element_type=jnp.float32,
    )
    hidden = jnp.maximum(preact, 0.0).astype(jnp.bfloat16)
    outputs = jnp.dot(hidden, w_second[0], preferred_element_type=jnp.float32).astype(jnp.bfloat16)
    width = outputs.shape[1]
    share = my_rows // towers
    gathered = lax.all_to_all(
        outputs.reshape(1, towers, share, width), "tower", split_axis=1, concat_axis=0, tiled=True
    )[:, 0]
    amount = gathered.shape[1]
    joined = jnp.transpose(gathered, (1, 0, 2)).reshape(amount, towers * width)
    head = jnp.dot(joined, w_head, preferred_element_type=jnp.float32)
    widened = gathered.astype(jnp.float32)
    products = jnp.einsum(
        "tmz,smz->mts", widened, widened, precision=lax.Precision.HIGHEST
    ) / math.sqrt(width)
    interact_term = jnp.dot(
        products.reshape(amount, towers * towers), w_interact, precision=lax.Precision.HIGHEST
    )
    scored = head + interact_term
    return scored[None]


def solution(mesh):
    return jax.shard_map(
        on_device,
        mesh=mesh,
        in_specs=(
            P("tower", "dev", None, None),
            P("tower", "dev", None, None),
            P(),
            P("tower", "dev", None),
            P("tower", None, None),
            P(),
            P(),
        ),
        out_specs=P("dev", "tower", None),
        check_vma=False,
    )
```

profile of v0, /device:TPU:1, one launch (start us, length us, event | category | flops | bytes accessed | tf_op | source)
XLA Modules:
  0.0 118.9 jit_solution(7275496688290093356)
XLA Ops:
  6.5 0.0 copy-start
  6.5 0.7 all-gather.3.cloned.1.call-update
  7.3 2.3 %copy.17 = s32[1,1,2048,32]{3,2,1,0:T(8,128)} copy(s32[1,1,2048,32]{2,3,1,0:T(8,128)} %param.9) | data formatting | bytes 524288 | tf_op args[0]
  9.5 0.7 fusion.27
  10.2 53.5 %while.11 = (s32[]{:T(128)}, bf16[4,512,128]{2,1,0:T(8,128)(2,1)S(1)}, s32[4,512,32]{2,1,0:T(8,128)}, bf16[512,128]{1,0:T(8,128)(2,1)}, s32[]{:T(128)}) while((s32[]{:T(128)}, bf16[4,512,128]{2,1,0:T(8,128)(2,1)S(1)}, s32[4,512,32]{2,1,0:T(8,128)}, bf16[512,128]{1,0:T(8,128)(2,1)}, s32[]{:T(128)}) %tuple.27), condition=%wide.region_2.3_spmd.clone, body=%wide.region_0.2_spmd.clone.sunk | while | flops 92340224 | bytes 2555973 | solution.py:22
  10.2 1.0 dynamic-slice_bitcast_fusion.2
  11.2 11.1 %convert_reduce_fusion.2 = s32[512,512]{1,0:T(8,128)S(1)} fusion(s32[512,32]{1,0:T(8,128)S(1)} %dynamic-slice_bitcast_fusion.2), kind=kLoop, calls=%fused_computation.3.clone.1 | loop fusion | flops 24903680 | bytes 1114112 | tf_op jit(solution)/shard_map/while/body/eval_jaxpr/reduce_sum | solution.py:17
  22.4 1.3 %fusion.41 = bf16[4,512,128]{2,1,0:T(8,128)(2,1)S(1)} fusion(bf16[4,512,128]{2,1,0:T(8,128)(2,1)S(1)} %get-tuple-element.82, s32[]{:T(128)} %get-tuple-element.81, bf16[512,128]{1,0:T(8,128)(2,1)} %get-tuple-element.89, s32[512,512]{1,0:T(8,128)S(1)} %convert_reduce_fusion.2), kind=kOutput, calls=%fused_computation.6.clone.1 | convolution fusion | flops 67436544 | bytes 1310724 | tf_op jit(solution)/shard_map/while/body/eval_jaxpr/dot_general | solution.py:18
  23.6 1.0 dynamic-slice_bitcast_fusion.2
  24.6 11.1 %convert_reduce_fusion.2 = s32[512,512]{1,0:T(8,128)S(1)} fusion(s32[512,32]{1,0:T(8,128)S(1)} %dynamic-slice_bitcast_fusion.2), kind=kLoop, calls=%fused_computation.3.clone.1 | loop fusion | flops 24903680 | bytes 1114112 | tf_op jit(solution)/shard_map/while/body/eval_jaxpr/reduce_sum | solution.py:17
  35.7 1.3 %fusion.41 = bf16[4,512,128]{2,1,0:T(8,128)(2,1)S(1)} fusion(bf16[4,512,128]{2,1,0:T(8,128)(2,1)S(1)} %get-tuple-element.82, s32[]{:T(128)} %get-tuple-element.81, bf16[512,128]{1,0:T(8,128)(2,1)} %get-tuple-element.89, s32[512,512]{1,0:T(8,128)S(1)} %convert_reduce_fusion.2), kind=kOutput, calls=%fused_computation.6.clone.1 | convolution fusion | flops 67436544 | bytes 1310724 | tf_op jit(solution)/shard_map/while/body/eval_jaxpr/dot_general | solution.py:18
  37.0 1.0 dynamic-slice_bitcast_fusion.2
  38.0 11.1 %convert_reduce_fusion.2 = s32[512,512]{1,0:T(8,128)S(1)} fusion(s32[512,32]{1,0:T(8,128)S(1)} %dynamic-slice_bitcast_fusion.2), kind=kLoop, calls=%fused_computation.3.clone.1 | loop fusion | flops 24903680 | bytes 1114112 | tf_op jit(solution)/shard_map/while/body/eval_jaxpr/reduce_sum | solution.py:17
  49.1 1.3 %fusion.41 = bf16[4,512,128]{2,1,0:T(8,128)(2,1)S(1)} fusion(bf16[4,512,128]{2,1,0:T(8,128)(2,1)S(1)} %get-tuple-element.82, s32[]{:T(128)} %get-tuple-element.81, bf16[512,128]{1,0:T(8,128)(2,1)} %get-tuple-element.89, s32[512,512]{1,0:T(8,128)S(1)} %convert_reduce_fusion.2), kind=kOutput, calls=%fused_computation.6.clone.1 | convolution fusion | flops 67436544 | bytes 1310724 | tf_op jit(solution)/shard_map/while/body/eval_jaxpr/dot_general | solution.py:18
  50.4 1.0 dynamic-slice_bitcast_fusion.2
  51.4 11.1 %convert_reduce_fusion.2 = s32[512,512]{1,0:T(8,128)S(1)} fusion(s32[512,32]{1,0:T(8,128)S(1)} %dynamic-slice_bitcast_fusion.2), kind=kLoop, calls=%fused_computation.3.clone.1 | loop fusion | flops 24903680 | bytes 1114112 | tf_op jit(solution)/shard_map/while/body/eval_jaxpr/reduce_sum | solution.py:17
  62.5 1.3 %fusion.41 = bf16[4,512,128]{2,1,0:T(8,128)(2,1)S(1)} fusion(bf16[4,512,128]{2,1,0:T(8,128)(2,1)S(1)} %get-tuple-element.82, s32[]{:T(128)} %get-tuple-element.81, bf16[512,128]{1,0:T(8,128)(2,1)} %get-tuple-element.89, s32[512,512]{1,0:T(8,128)S(1)} %convert_reduce_fusion.2), kind=kOutput, calls=%fused_computation.6.clone.1 | convolution fusion | flops 67436544 | bytes 1310724 | tf_op jit(solution)/shard_map/while/body/eval_jaxpr/dot_general | solution.py:18
  63.8 0.0 copy-start.2
  63.8 6.2 %gather_fusion = bf16[2048,128]{1,0:T(8,128)(2,1)S(1)} fusion(bf16[2048,128]{1,0:T(8,128)(2,1)S(1)} %bitcast.58, s32[2048]{0:T(1024)S(1)} %fusion.27), kind=kCustom, calls=%fused_computation | custom fusion | bytes 1056768 | tf_op jit(solution)/shard_map/jit(_take)/gather | solution.py:32
  70.0 0.3 copy.18
  70.3 0.0 copy-done.2
  70.3 0.1 broadcast_select_fusion
  70.4 16.4 %all_to_all.25 = bf16[16,128,128]{1,2,0:T(8,128)(2,1)S(1)} all-to-all(bf16[16,128,128]{1,2,0:T(8,128)(2,1)S(1)} %broadcast_select_fusion), channel_id=1, replica_groups=mesh['tower'=16,'dev'=16] {'dev'}, dimensions={0} | all-to-all | bytes 1048576 | tf_op jit(solution)/shard_map/all_to_all | solution.py:33
  86.8 3.5 %fusion.19 = bf16[1,16,8,512]{3,2,0,1:T(8,128)(2,1)S(1)} fusion(bf16[128,2048]{0,1:T(8,128)(2,1)S(1)} %bitcast.61, bf16[1,2048,1024]{2,1,0:T(8,128)(2,1)} %all-gather.3.cloned.1.call-done, bf16[1,1024,512]{2,1,0:T(8,128)(2,1)} %param.13), kind=kOutput, calls=%fused_computation.15 | convolution fusion | flops 671416320 | bytes 5898240 | tf_op jit(solution)/shard_map/dot_general | solution.py:40
  90.2 20.2 %all_to_all.26 = bf16[1,16,8,512]{3,2,0,1:T(8,128)(2,1)S(1)} all-to-all(bf16[1,16,8,512]{3,2,0,1:T(8,128)(2,1)S(1)} %fusion.19), channel_id=1, replica_groups=mesh['tower'=16,'dev'=16] {'tower'}, dimensions={1} | all-to-all | bytes 262144 | tf_op jit(solution)/shard_map/all_to_all | solution.py:43
  110.5 0.1 copy.21
  110.6 0.2 convolution_multiply_fusion
  110.8 0.1 reshape.35
  110.9 0.0 copy-done
  110.9 0.4 fusion.29
  111.3 0.0 copy-done.1
  111.3 0.8 fusion.22
  (6 shorter events, 0.1 us)
Async XLA Ops:
  6.5 104.3 %copy-start = (bf16[8192,128]{1,0:T(8,128)(2,1)S(1)}, bf16[8192,128]{1,0:T(8,128)(2,1)}, u32[]{:S(2)}) copy-start(bf16[8192,128]{1,0:T(8,128)(2,1)} %param.14) | copy-start | bytes 6291460
  6.5 80.2 %all-gather.3.cloned.1.call-start = ((), (), s32[]{:S(2)}) async-start(), calls=%async_computation.2 | async-start | bytes 4456448 | tf_op jit(solution)/shard_map/all_gather | solution.py:36
  63.8 6.5 %copy-start.2 = (s32[2048]{0:T(1024)S(1)}, s32[2048]{0:T(1024)}, u32[]{:S(2)}) copy-start(s32[2048]{0:T(1024)} %param.11) | copy-start | bytes 24580
  86.8 24.5 %copy-start.1 = (f32[256,128]{1,0:T(8,128)S(1)}, f32[256,128]{1,0:T(8,128)}, u32[]{:S(2)}) copy-start(f32[256,128]{1,0:T(8,128)} %param.15) | copy-start | bytes 393220
Sparse Core Ops, SparseCore 0:
  9.2 43.9 all-gather.2
where the time goes:
time: 119 us
  other arithmetic  45.3 us (38%)
  blocking collectives  36.6 us (31%)
  between operations  13.5 us (11%)
  local copies, waits for them, and re-layouts  12.9 us (11%)
  matrix products  9.84 us (8%)
    reduce_sum x4, other arithmetic, pool_block(): jnp.sum((block_ids[:, :, None] == positions).astype(jnp.int32), axis=1)  44.5 us
    all_to_all x1, blocking collectives, on_device(): lax.all_to_all(outputs.reshape(1, towers, share, width), 'tower', split_a...  20.2 us
    all_to_all x1, blocking collectives, on_device(): lax.all_to_all(features, 'dev', split_axis=0, concat_axis=1, tiled=True)  16.4 us
    gather x2, local copies, waits for them, and re-layouts, on_device(): features = jnp.take(pieces, order, axis=0)  6.47 us
    dot_general x4, matrix products, pool_block(): jnp.dot(tally.astype(jnp.bfloat16), table, preferred_element_type=jnp.flo...  5.05 us
    eq x4, local copies, waits for them, and re-layouts, pool_block(): block_ids[:, :, None] == positions  3.88 us
    dot_general x1, matrix products, on_device(): jnp.dot(hidden, w_second[0], preferred_element_type=jnp.float32)  3.47 us
  transfers between devices with their start and end apart: 1, of which 0 were waited for; matrix products, arithmetic and copies ran while one was open for 53% of the time, Pallas kernels for 0%

commit v1 on v0

v1 whole, which is shorter than its diff:
```python
import functools
import math

import jax
import jax.numpy as jnp
from jax import lax
from jax.experimental import pallas as pl
from jax.experimental.pallas import tpu as pltpu
from jax.sharding import PartitionSpec as P

MESH = pl.DeviceIdType.MESH
RING = 4
CORES = 2


def load(src, dst, sem):
    return pltpu.make_async_copy(src, dst, sem)


def pool(ids_ref, table_ref, pooled_ref):
    bag, samples = ids_ref.shape
    active = table_ref.shape[0]
    lanes = 128
    fields = active // lanes
    places = lax.broadcasted_iota(jnp.int32, (lanes, lanes), 0)

    def chunk(index, carry):
        start = pl.multiple_of(index * lanes, lanes)
        packed = jnp.zeros((lanes, lanes), jnp.int32)
        for j in range(bag):
            row = ids_ref[pl.ds(j, 1), pl.ds(start, lanes)]
            low = row & (lanes - 1)
            unit = jnp.left_shift(1, (row >> 7) << 3)
            packed = packed + jnp.where(low == places, unit, 0)
        turned = packed.T
        counts = jnp.concatenate(
            [
                ((turned >> (8 * field)) & 255).astype(jnp.float32).astype(jnp.bfloat16)
                for field in range(fields)
            ],
            axis=1,
        )
        pooled_ref[pl.ds(start, lanes), :] = jnp.dot(
            counts, table_ref[...], preferred_element_type=jnp.float32
        )
        return carry

    lax.fori_loop(0, samples // lanes, chunk, 0)


def kernel(
    ids_hbm,
    table_hbm,
    order_ref,
    first_hbm,
    second_hbm,
    head_hbm,
    inter_hbm,
    out_ref,
    ids_v,
    table_v,
    pooled,
    permuted,
    xsend,
    wbuf,
    xbuf,
    total,
    partial,
    second_v,
    outbox,
    inbox,
    head_v,
    inter_v,
    spread_hi,
    spread_lo,
    load_sem,
    w_send,
    w_recv,
    x_send,
    x_recv,
    p_send,
    p_recv,
    o_send,
    o_recv,
    towers,
    chips,
):
    tower = lax.axis_index("tower")
    dev = lax.axis_index("dev")
    core = lax.rem(dev, CORES)
    chip = dev // CORES
    col = chip // RING
    row = lax.rem(chip, RING)
    cols = chips // RING
    partner = dev + 1 - 2 * core

    def shifted(step, sign):
        dx, dy = step // RING, lax.rem(step, RING)
        return lax.rem(col + cols + sign * dx, cols) * RING + lax.rem(row + RING + sign * dy, RING)

    loads = [
        load(ids_hbm, ids_v, load_sem.at[0]),
        load(table_hbm, table_v, load_sem.at[1]),
        load(first_hbm, wbuf.at[chip], load_sem.at[2]),
        load(second_hbm, second_v, load_sem.at[3]),
        load(head_hbm, head_v, load_sem.at[4]),
        load(inter_hbm, inter_v, load_sem.at[5]),
    ]
    for copy in loads:
        copy.start()

    barrier = pltpu.get_barrier_semaphore()
    for step in range(1, towers):
        pl.semaphore_signal(
            barrier, inc=1, device_id={"tower": lax.rem(tower + step, towers)}, device_id_type=MESH
        )
    for step in range(1, chips):
        pl.semaphore_signal(
            barrier, inc=1, device_id={"dev": shifted(step, 1) * CORES + core}, device_id_type=MESH
        )
    pl.semaphore_signal(barrier, inc=1, device_id={"dev": partner}, device_id_type=MESH)

    loads[0].wait()
    loads[1].wait()
    pool(ids_v, table_v, pooled)
    loads[2].wait()
    pl.semaphore_wait(barrier, towers + chips - 1)

    def send_w(step):
        return pltpu.make_async_remote_copy(
            src_ref=wbuf.at[chip],
            dst_ref=wbuf.at[chip],
            send_sem=w_send.at[step],
            recv_sem=w_recv.at[chip],
            device_id={"dev": shifted(step, 1) * CORES + core},
            device_id_type=MESH,
        )

    def send_x(step):
        return pltpu.make_async_remote_copy(
            src_ref=xsend.at[shifted(step, 1)],
            dst_ref=xbuf.at[chip],
            send_sem=x_send.at[step],
            recv_sem=x_recv.at[chip],
            device_id={"dev": shifted(step, 1) * CORES + core},
            device_id_type=MESH,
        )

    for step in range(1, chips):
        send_w(step).start()

    rows = xsend.shape[1]

    def permute_block(block):
        def group(index, carry):
            base = block * rows + index * 16
            for q in range(16):
                source = order_ref[base + q]
                permuted[pl.ds(index * 16 + q, 1), :] = pooled[pl.ds(source, 1), :]
            return carry

        lax.fori_loop(0, rows // 16, group, 0)
        xsend[block] = permuted[...].astype(jnp.bfloat16)

    for step in range(1, chips):
        permute_block(shifted(step, 1))
        send_x(step).start()
    permute_block(chip)

    loads[5].wait()
    half_k = inter_v.shape[0]

    def widen(index, carry):
        start = pl.multiple_of(index * 16, 16)
        block = inter_v[pl.ds(start, 16), :]
        wide = jnp.broadcast_to(block[:, None, :], (16, 8, block.shape[1])).reshape(
            128, block.shape[1]
        )
        high = wide.astype(jnp.bfloat16)
        low = (wide - high.astype(jnp.float32)).astype(jnp.bfloat16)
        target = pl.multiple_of(index * 128, 128)
        spread_hi[pl.ds(target, 128), :] = high
        spread_lo[pl.ds(target, 128), :] = low
        return carry

    lax.fori_loop(0, half_k // 16, widen, 0)

    width = total.shape[2]
    tile = 256

    def product(x, w, first):
        for n in range(width // tile):
            part = jnp.dot(
                x, w[:, n * tile : (n + 1) * tile], preferred_element_type=jnp.float32
            ).reshape(2, rows // 2, tile)
            span = slice(n * tile, (n + 1) * tile)
            if first:
                total[:, :, span] = part
            else:
                total[:, :, span] += part

    product(xsend[chip], wbuf.at[chip], True)

    def arrive(step, carry):
        source = shifted(step, -1)
        pltpu.make_async_remote_copy(
            src_ref=wbuf.at[source],
            dst_ref=wbuf.at[source],
            send_sem=w_send.at[step],
            recv_sem=w_recv.at[source],
            device_id={"dev": partner},
            device_id_type=MESH,
        ).wait_recv()
        pltpu.make_async_remote_copy(
            src_ref=xbuf.at[source],
            dst_ref=xbuf.at[source],
            send_sem=x_send.at[step],
            recv_sem=x_recv.at[source],
            device_id={"dev": partner},
            device_id_type=MESH,
        ).wait_recv()
        product(xbuf[source], wbuf.at[source], False)
        return carry

    lax.fori_loop(1, chips, arrive, 0)

    swap = pltpu.make_async_remote_copy(
        src_ref=total.at[1 - core],
        dst_ref=partial,
        send_sem=p_send,
        recv_sem=p_recv,
        device_id={"dev": partner},
        device_id_type=MESH,
    )
    swap.start()
    loads[3].wait()
    swap.wait_recv()
    hidden = jnp.maximum(total[core] + partial[...], 0.0).astype(jnp.bfloat16)
    outputs = jnp.dot(hidden, second_v[...], preferred_element_type=jnp.float32)
    share = outbox.shape[1]
    outbox[...] = outputs.reshape(towers, share, outputs.shape[1]).astype(jnp.bfloat16)

    def send_o(step):
        peer = lax.rem(tower + step, towers)
        return pltpu.make_async_remote_copy(
            src_ref=outbox.at[peer],
            dst_ref=inbox.at[tower],
            send_sem=o_send.at[step],
            recv_sem=o_recv.at[tower],
            device_id={"tower": peer},
            device_id_type=MESH,
        )

    for step in range(1, towers):
        send_o(step).start()
    inbox[tower] = outbox[tower]
    loads[4].wait()

    def head_part(source):
        return jnp.dot(inbox[source], head_v[source], preferred_element_type=jnp.float32)

    def collect(step, value):
        source = lax.rem(tower + towers - step, towers)
        pltpu.make_async_remote_copy(
            src_ref=outbox.at[source],
            dst_ref=inbox.at[source],
            send_sem=o_send.at[step],
            recv_sem=o_recv.at[source],
            device_id={"dev": partner},
            device_id_type=MESH,
        ).wait_recv()
        return value + head_part(source)

    head = lax.fori_loop(1, towers, collect, head_part(tower))

    zwidth = inbox.shape[2]
    stacked = (
        inbox[...].astype(jnp.float32).reshape(towers * share, zwidth).astype(jnp.bfloat16)
    )
    gram = lax.dot_general(
        stacked, stacked, (((1,), (1,)), ((), ())), preferred_element_type=jnp.float32
    )
    left = lax.rem(lax.broadcasted_iota(jnp.int32, gram.shape, 0), share)
    right = lax.rem(lax.broadcasted_iota(jnp.int32, gram.shape, 1), share)
    gram = jnp.where(left == right, gram / math.sqrt(zwidth), 0.0)
    flat = jnp.concatenate(
        [gram[t * share : (t + 1) * share, :] for t in range(towers)], axis=1
    )
    flat_hi = flat.astype(jnp.bfloat16)
    flat_lo = (flat - flat_hi.astype(jnp.float32)).astype(jnp.bfloat16)
    interact = (
        jnp.dot(flat_hi, spread_hi[...], preferred_element_type=jnp.float32)
        + jnp.dot(flat_lo, spread_hi[...], preferred_element_type=jnp.float32)
        + jnp.dot(flat_hi, spread_lo[...], preferred_element_type=jnp.float32)
    )
    out_ref[...] = head + interact

    for step in range(1, chips):
        send_w(step).wait_send()
        send_x(step).wait_send()
    swap.wait_send()
    for step in range(1, towers):
        send_o(step).wait_send()


def on_device(ids, tables, order, w_first, w_second, w_head, w_interact):
    towers = lax.axis_size("tower")
    chips = lax.axis_size("dev") // CORES
    samples, bag = ids.shape[2:]
    active, emb = tables.shape[2:]
    hidden = w_first.shape[2]
    zwidth = w_second.shape[2]
    heads = w_head.shape[1]
    rows = samples // chips
    share = rows // CORES // towers
    pairs = w_interact.shape[0]
    vmem = pltpu.VMEM
    dma = pltpu.SemaphoreType.DMA
    anywhere = pl.BlockSpec(memory_space=pl.ANY)
    scores = pl.pallas_call(
        functools.partial(kernel, towers=towers, chips=chips),
        out_shape=jax.ShapeDtypeStruct((share, heads), jnp.float32),
        in_specs=[
            anywhere,
            anywhere,
            pl.BlockSpec(memory_space=pltpu.SMEM),
            anywhere,
            anywhere,
            anywhere,
            anywhere,
        ],
        out_specs=pl.BlockSpec(memory_space=vmem),
        scratch_shapes=[
            vmem((bag, samples), jnp.int32),
            vmem((active, emb), jnp.bfloat16),
            vmem((samples, emb), jnp.float32),
            vmem((rows, emb), jnp.float32),
            vmem((chips, rows, emb), jnp.bfloat16),
            vmem((chips, emb, hidden), jnp.bfloat16),
            vmem((chips, rows, emb), jnp.bfloat16),
            vmem((CORES, rows // CORES, hidden), jnp.float32),
            vmem((rows // CORES, hidden), jnp.float32),
            vmem((hidden, zwidth), jnp.bfloat16),
            vmem((towers, share, zwidth), jnp.bfloat16),
            vmem((towers, share, zwidth), jnp.bfloat16),
            vmem((towers, zwidth, heads), jnp.bfloat16),
            vmem((pairs, heads), jnp.float32),
            vmem((pairs * share, heads), jnp.bfloat16),
            vmem((pairs * share, heads), jnp.bfloat16),
            dma((6,)),
            dma((chips,)),
            dma((chips,)),
            dma((chips,)),
            dma((chips,)),
            dma,
            dma,
            dma((towers,)),
            dma((towers,)),
        ],
        compiler_params=pltpu.CompilerParams(
            collective_id=0, has_side_effects=True, vmem_limit_bytes=48 * 1024 * 1024
        ),
    )(
        jnp.swapaxes(ids[0, 0], 0, 1),
        tables[0, 0],
        order,
        w_first[0],
        w_second[0],
        w_head.reshape(towers, zwidth, heads),
        w_interact,
    )
    return scores[None]


def solution(mesh):
    return jax.shard_map(
        on_device,
        mesh=mesh,
        in_specs=(
            P("tower", "dev", None, None),
            P("tower", "dev", None, None),
            P(),
            P("tower", "dev", None),
            P("tower", None, None),
            P(),
            P(),
        ),
        out_specs=P("dev", "tower", None),
        check_vma=False,
    )
```

time: 119 us -> 68.2 us (0.57)
  Pallas kernels: 0 us -> 60.1 us
  other arithmetic: 45.3 us -> 0 us
  blocking collectives: 36.6 us -> 0 us
  between operations: 13.5 us -> 0.02 us
  matrix products: 9.84 us -> 0 us
  local copies, waits for them, and re-layouts: 12.9 us -> 7.81 us
    pallas_call x0 -> x1, Pallas kernels: none -> 60.1 us  [on_device(): pl.pallas_call(functools.partial(kernel, towers=towers, chips=chips), out...]
    reduce_sum x4 -> x0, other arithmetic: 44.5 us -> none  [pool_block(): jnp.sum((block_ids[:, :, None] == positions).astype(jnp.int32), axis=1)]
    all_to_all x2 -> x0, blocking collectives: 36.6 us -> none  [the longest x1 20.2 us: on_device(): lax.all_to_all(outputs.reshape(1, towers, share, width), 'tower', split_a...]
    dot_general x8 -> x0, matrix products: 9.84 us -> none  [the longest x4 5.05 us: pool_block(): jnp.dot(tally.astype(jnp.bfloat16), table, preferred_element_type=jnp.flo...]
    gather x2 -> x0, local copies, waits for them, and re-layouts: 6.47 us -> none  [on_device(): features = jnp.take(pieces, order, axis=0)]
    unnamed x8 -> x15, local copies, waits for them, and re-layouts: 2.37 us -> 7.81 us
    eq x4 -> x0, local copies, waits for them, and re-layouts: 3.88 us -> none  [pool_block(): block_ids[:, :, None] == positions]
  transfers between devices with their start and end apart: 1 -> 0, of which waited for: 0 -> 0; matrix products, arithmetic and copies ran while one was open for 53% -> 0% of each run, Pallas kernels for 0% -> 0%
where the time goes in v1:
time: 68.2 us; the launch traced here: 68 us
  Pallas kernels  60.1 us (88%)
  local copies, waits for them, and re-layouts  7.81 us (11%)
    pallas_call x1, Pallas kernels, on_device(): pl.pallas_call(functools.partial(kernel, towers=towers, chips=chips), out...  60.1 us
    unnamed x15, local copies, waits for them, and re-layouts  7.81 us

profile of v1, /device:TPU:1, one launch (start us, length us, event | category | flops | bytes accessed | tf_op | source)
XLA Modules:
  0.0 68.0 jit_solution(6344667941184650098)
XLA Ops:
  0.0 0.0 copy-start
  0.0 1.6 %copy-done = bf16[8192,128]{1,0:T(8,128)(2,1)S(1)} copy-done((bf16[8192,128]{1,0:T(8,128)(2,1)S(1)}, bf16[8192,128]{1,0:T(8,128)(2,1)}, u32[]{:S(2)}) %copy-start) | copy-done | bytes 2097176
  1.6 0.0 copy-start.1
  1.6 1.2 %copy-done.1 = bf16[1,1024,512]{2,1,0:T(8,128)(2,1)S(1)} copy-done((bf16[1,1024,512]{2,1,0:T(8,128)(2,1)S(1)}, bf16[1,1024,512]{2,1,0:T(8,128)(2,1)}, u32[]{:S(2)}) %copy-start.1) | copy-done | bytes 1048600
  2.8 0.0 copy-start.2
  2.8 0.9 %copy-done.2 = s32[1,1,2048,32]{2,3,1,0:T(8,128)S(1)} copy-done((s32[1,1,2048,32]{2,3,1,0:T(8,128)S(1)}, s32[1,1,2048,32]{2,3,1,0:T(8,128)}, u32[]{:S(2)}) %copy-start.2) | copy-done | bytes 262168
  3.8 0.0 copy-start.3
  3.8 0.9 %copy-done.3 = bf16[1,128,1024]{2,1,0:T(8,128)(2,1)S(1)} copy-done((bf16[1,128,1024]{2,1,0:T(8,128)(2,1)S(1)}, bf16[1,128,1024]{2,1,0:T(8,128)(2,1)}, u32[]{:S(2)}) %copy-start.3) | copy-done | bytes 262168
  4.7 0.0 copy-start.4
  4.7 0.9 %copy-done.4 = bf16[1,1,512,128]{3,2,1,0:T(8,128)(2,1)S(1)} copy-done((bf16[1,1,512,128]{3,2,1,0:T(8,128)(2,1)S(1)}, bf16[1,1,512,128]{3,2,1,0:T(8,128)(2,1)}, u32[]{:S(2)}) %copy-start.4) | copy-done | bytes 131096
  5.6 0.0 copy-start.5
  5.6 0.9 %copy-done.5 = f32[256,128]{1,0:T(8,128)S(1)} copy-done((f32[256,128]{1,0:T(8,128)S(1)}, f32[256,128]{1,0:T(8,128)}, u32[]{:S(2)}) %copy-start.5) | copy-done | bytes 131096
  6.5 0.0 copy-start.6
  6.5 0.7 %copy-done.6 = s32[2048]{0:T(1024)S(1)} copy-done((s32[2048]{0:T(1024)S(1)}, s32[2048]{0:T(1024)}, u32[]{:S(2)}) %copy-start.6) | copy-done | bytes 8216
  7.2 60.1 %shard_map.73 = f32[8,128]{1,0:T(8,128)S(1)} custom-call(s32[32,2048]{1,0:T(8,128)S(1)} %bitcast.10, bf16[512,128]{1,0:T(8,128)(2,1)S(1)} %bitcast.12, s32[2048]{0:T(1024)S(1)} %copy-done.6, bf16[128,1024]{1,0:T(8,128)(2,1)S(1)} %bitcast.11, bf16[1024,512]{1,0:T(8,128)(2,1)S(1)} %bitcast.9, bf16[16,512,128]{2,1,0:T(8,128)(2,1)S(1)} %bitcast.8, ...), custom_call_target="tpu_custom_call" | custom-call | tf_op jit(solution)/shard_map/pallas_call | solution.py:320
  67.4 0.6 copy.9
Async XLA Ops:
  0.0 1.6 %copy-start = (bf16[8192,128]{1,0:T(8,128)(2,1)S(1)}, bf16[8192,128]{1,0:T(8,128)(2,1)}, u32[]{:S(2)}) copy-start(bf16[8192,128]{1,0:T(8,128)(2,1)} %param.12) | copy-start | bytes 6291460
  1.6 1.2 %copy-start.1 = (bf16[1,1024,512]{2,1,0:T(8,128)(2,1)S(1)}, bf16[1,1024,512]{2,1,0:T(8,128)(2,1)}, u32[]{:S(2)}) copy-start(bf16[1,1024,512]{2,1,0:T(8,128)(2,1)} %param.11) | copy-start | bytes 3145732
  2.8 0.9 %copy-start.2 = (s32[1,1,2048,32]{2,3,1,0:T(8,128)S(1)}, s32[1,1,2048,32]{2,3,1,0:T(8,128)}, u32[]{:S(2)}) copy-start(s32[1,1,2048,32]{2,3,1,0:T(8,128)} %param.7) | copy-start | bytes 786436
  3.8 0.9 %copy-start.3 = (bf16[1,128,1024]{2,1,0:T(8,128)(2,1)S(1)}, bf16[1,128,1024]{2,1,0:T(8,128)(2,1)}, u32[]{:S(2)}) copy-start(bf16[1,128,1024]{2,1,0:T(8,128)(2,1)} %param.10) | copy-start | bytes 786436
  4.7 0.9 %copy-start.4 = (bf16[1,1,512,128]{3,2,1,0:T(8,128)(2,1)S(1)}, bf16[1,1,512,128]{3,2,1,0:T(8,128)(2,1)}, u32[]{:S(2)}) copy-start(bf16[1,1,512,128]{3,2,1,0:T(8,128)(2,1)} %param.8) | copy-start | bytes 393220
  5.6 0.9 %copy-start.5 = (f32[256,128]{1,0:T(8,128)S(1)}, f32[256,128]{1,0:T(8,128)}, u32[]{:S(2)}) copy-start(f32[256,128]{1,0:T(8,128)} %inter_hbm.1) | copy-start | bytes 393220
  6.5 0.7 %copy-start.6 = (s32[2048]{0:T(1024)S(1)}, s32[2048]{0:T(1024)}, u32[]{:S(2)}) copy-start(s32[2048]{0:T(1024)} %order_ref.1) | copy-start | bytes 24580

commit v2 on v1

v2 whole, which is shorter than its diff:
```python
import functools
import math

import jax
import jax.numpy as jnp
from jax import lax
from jax.experimental import pallas as pl
from jax.experimental.pallas import tpu as pltpu
from jax.sharding import PartitionSpec as P

MESH = pl.DeviceIdType.MESH
RING = 4
CORES = 2
CHUNKS = 4


def pool(ids_ref, table_ref, pooled_ref):
    bag, samples = ids_ref.shape
    active = table_ref.shape[0]
    lanes = 128
    fields = active // lanes
    places = lax.broadcasted_iota(jnp.int32, (lanes, lanes), 0)

    def chunk(index, carry):
        start = pl.multiple_of(index * lanes, lanes)
        packed = jnp.zeros((lanes, lanes), jnp.int32)
        for j in range(bag):
            row = ids_ref[pl.ds(j, 1), pl.ds(start, lanes)]
            low = row & (lanes - 1)
            unit = jnp.left_shift(1, (row >> 7) << 3)
            packed = packed + jnp.where(low == places, unit, 0)
        turned = packed.T
        counts = jnp.concatenate(
            [
                ((turned >> (8 * field)) & 255).astype(jnp.float32).astype(jnp.bfloat16)
                for field in range(fields)
            ],
            axis=1,
        )
        pooled_ref[pl.ds(start, lanes), :] = jnp.dot(
            counts, table_ref[...], preferred_element_type=jnp.float32
        )
        return carry

    lax.fori_loop(0, samples // lanes, chunk, 0)


def kernel(
    ids_hbm,
    table_hbm,
    order_ref,
    first_hbm,
    second_hbm,
    head_hbm,
    inter_hbm,
    out_ref,
    ids_v,
    table_v,
    pooled,
    permuted,
    xsend,
    xall,
    wall,
    total,
    cross,
    relay,
    final,
    outsum,
    second_v,
    outbox,
    inbox,
    head_v,
    inter_v,
    spread_hi,
    spread_lo,
    load_sem,
    first_sem,
    w_send,
    w_recv,
    x_send,
    x_recv,
    c_send,
    c_recv,
    f_send,
    f_recv,
    o_send,
    o_recv,
    towers,
):
    tower = lax.axis_index("tower")
    dev = lax.axis_index("dev")
    core = lax.rem(dev, CORES)
    chip = dev // CORES
    col = chip // RING
    row = lax.rem(chip, RING)
    chunks, _, tile = wall.shape
    emb = table_v.shape[1]
    block = permuted.shape[0]

    def along(step):
        return lax.rem(row + step, RING)

    def at_row(place):
        return {"dev": (col * RING + place) * CORES + core}

    partner = {"dev": dev + 1 - 2 * core}
    across = {"dev": ((1 - col) * RING + row) * CORES + core}

    mine = pl.ds(pl.multiple_of(row * emb, emb), emb)
    loads = [
        pltpu.make_async_copy(ids_hbm, ids_v, load_sem.at[0]),
        pltpu.make_async_copy(table_hbm, table_v, load_sem.at[1]),
        pltpu.make_async_copy(second_hbm, second_v, load_sem.at[2]),
        pltpu.make_async_copy(head_hbm, head_v, load_sem.at[3]),
        pltpu.make_async_copy(inter_hbm, inter_v, load_sem.at[4]),
    ]
    firsts = [
        pltpu.make_async_copy(
            first_hbm.at[:, pl.ds(n * tile, tile)], wall.at[n, mine, :], first_sem.at[n]
        )
        for n in range(chunks)
    ]
    loads[0].start()
    loads[1].start()
    for copy in firsts:
        copy.start()
    for copy in loads[2:]:
        copy.start()

    barrier = pltpu.get_barrier_semaphore()
    for step in range(1, towers):
        pl.semaphore_signal(
            barrier, inc=1, device_id={"tower": lax.rem(tower + step, towers)}, device_id_type=MESH
        )
    for step in range(1, RING):
        pl.semaphore_signal(barrier, inc=1, device_id=at_row(along(step)), device_id_type=MESH)
    pl.semaphore_signal(barrier, inc=1, device_id=partner, device_id_type=MESH)
    pl.semaphore_signal(barrier, inc=1, device_id=across, device_id_type=MESH)

    loads[0].wait()
    loads[1].wait()
    pool(ids_v, table_v, pooled)
    for copy in firsts:
        copy.wait()
    pl.semaphore_wait(barrier, towers - 1 + RING - 1 + 2)

    steps = (1, 3, 2)

    def send_w(n, step):
        return pltpu.make_async_remote_copy(
            src_ref=wall.at[n, mine, :],
            dst_ref=wall.at[n, mine, :],
            send_sem=w_send.at[n, step],
            recv_sem=w_recv.at[n, row],
            device_id=at_row(along(step)),
            device_id_type=MESH,
        )

    def send_x(step):
        return pltpu.make_async_remote_copy(
            src_ref=xsend.at[along(step)],
            dst_ref=xall.at[:, mine],
            send_sem=x_send.at[step],
            recv_sem=x_recv.at[row],
            device_id=at_row(along(step)),
            device_id_type=MESH,
        )

    def permute_rows(place, store):
        for c in range(CORES):
            for x in range(2):
                start = ((x * RING + place) * CORES + c) * block

                def group(index, carry):
                    for q in range(16):
                        source = order_ref[start + index * 16 + q]
                        permuted[pl.ds(index * 16 + q, 1), :] = pooled[pl.ds(source, 1), :]
                    return carry

                lax.fori_loop(0, block // 16, group, 0)
                store(c * 2 + x, permuted[...].astype(jnp.bfloat16))

    for step in steps:
        send_w(0, step).start()
    for step in steps:
        place = along(step)

        def keep(part, value):
            xsend[place, part * block : (part + 1) * block, :] = value

        permute_rows(place, keep)
        send_x(step).start()
    for n in range(1, chunks):
        for step in steps:
            send_w(n, step).start()

    def keep_own(part, value):
        xall[part * block : (part + 1) * block, mine] = value

    permute_rows(row, keep_own)

    loads[4].wait()
    pairs = inter_v.shape[0]

    def widen(index, carry):
        start = pl.multiple_of(index * 16, 16)
        some = inter_v[pl.ds(start, 16), :]
        wide = jnp.broadcast_to(some[:, None, :], (16, 8, some.shape[1])).reshape(
            128, some.shape[1]
        )
        high = wide.astype(jnp.bfloat16)
        low = (wide - high.astype(jnp.float32)).astype(jnp.bfloat16)
        target = pl.multiple_of(index * 128, 128)
        spread_hi[pl.ds(target, 128), :] = high
        spread_lo[pl.ds(target, 128), :] = low
        return carry

    lax.fori_loop(0, pairs // 16, widen, 0)
    loads[2].wait()
    loads[3].wait()

    def arrived_w(n, step):
        source = along(step)
        span = pl.ds(pl.multiple_of(source * emb, emb), emb)
        return pltpu.make_async_remote_copy(
            src_ref=wall.at[n, span, :],
            dst_ref=wall.at[n, span, :],
            send_sem=w_send.at[n, step],
            recv_sem=w_recv.at[n, source],
            device_id=partner,
            device_id_type=MESH,
        )

    def arrived_x(step):
        source = along(step)
        span = pl.ds(pl.multiple_of(source * emb, emb), emb)
        return pltpu.make_async_remote_copy(
            src_ref=xsend.at[source],
            dst_ref=xall.at[:, span],
            send_sem=x_send.at[step],
            recv_sem=x_recv.at[source],
            device_id=partner,
            device_id_type=MESH,
        )

    def cross_copy(n):
        return pltpu.make_async_remote_copy(
            src_ref=total.at[n, 1 - core],
            dst_ref=cross.at[n],
            send_sem=c_send.at[n],
            recv_sem=c_recv.at[n],
            device_id=partner,
            device_id_type=MESH,
        )

    def final_copy(n):
        return pltpu.make_async_remote_copy(
            src_ref=relay.at[n],
            dst_ref=final.at[n],
            send_sem=f_send.at[n],
            recv_sem=f_recv.at[n],
            device_id=across,
            device_id_type=MESH,
        )

    def first_layer(n):
        if n == 0:
            for step in steps:
                arrived_x(step).wait_recv()
        for step in steps:
            arrived_w(n, step).wait_recv()
        part = jnp.dot(xall[...], wall[n], preferred_element_type=jnp.float32)
        total[n] = part.reshape(CORES, 2, block, tile)
        cross_copy(n).start()

    def add_cores(n):
        cross_copy(n).wait_recv()
        relay[n] = total[n, core, 1 - col] + cross[n, 1 - col]
        final_copy(n).start()

    def second_layer(n):
        final_copy(n).wait_recv()
        preact = total[n, core, col] + cross[n, col] + final[n]
        hidden = jnp.maximum(preact, 0.0).astype(jnp.bfloat16)
        part = jnp.dot(
            hidden, second_v[n * tile : (n + 1) * tile, :], preferred_element_type=jnp.float32
        )
        if n == 0:
            outsum[...] = part
        else:
            outsum[...] += part

    for n in range(chunks + 2):
        if n < chunks:
            first_layer(n)
        if 1 <= n <= chunks:
            add_cores(n - 1)
        if n >= 2:
            second_layer(n - 2)

    share = outbox.shape[1]
    outbox[...] = outsum[...].reshape(towers, share, outsum.shape[1]).astype(jnp.bfloat16)

    def send_o(step):
        peer = lax.rem(tower + step, towers)
        return pltpu.make_async_remote_copy(
            src_ref=outbox.at[peer],
            dst_ref=inbox.at[tower],
            send_sem=o_send.at[step],
            recv_sem=o_recv.at[tower],
            device_id={"tower": peer},
            device_id_type=MESH,
        )

    for step in range(1, towers):
        send_o(step).start()
    inbox[tower] = outbox[tower]

    def head_part(source):
        return jnp.dot(inbox[source], head_v[source], preferred_element_type=jnp.float32)

    def collect(step, value):
        source = lax.rem(tower + towers - step, towers)
        pltpu.make_async_remote_copy(
            src_ref=outbox.at[source],
            dst_ref=inbox.at[source],
            send_sem=o_send.at[step],
            recv_sem=o_recv.at[source],
            device_id=partner,
            device_id_type=MESH,
        ).wait_recv()
        return value + head_part(source)

    head = lax.fori_loop(1, towers, collect, head_part(tower))

    zwidth = inbox.shape[2]
    stacked = (
        inbox[...].astype(jnp.float32).reshape(towers * share, zwidth).astype(jnp.bfloat16)
    )
    gram = lax.dot_general(
        stacked, stacked, (((1,), (1,)), ((), ())), preferred_element_type=jnp.float32
    )
    left = lax.rem(lax.broadcasted_iota(jnp.int32, gram.shape, 0), share)
    right = lax.rem(lax.broadcasted_iota(jnp.int32, gram.shape, 1), share)
    gram = jnp.where(left == right, gram / math.sqrt(zwidth), 0.0)
    flat = jnp.concatenate(
        [gram[t * share : (t + 1) * share, :] for t in range(towers)], axis=1
    )
    flat_hi = flat.astype(jnp.bfloat16)
    flat_lo = (flat - flat_hi.astype(jnp.float32)).astype(jnp.bfloat16)
    interact = (
        jnp.dot(flat_hi, spread_hi[...], preferred_element_type=jnp.float32)
        + jnp.dot(flat_lo, spread_hi[...], preferred_element_type=jnp.float32)
        + jnp.dot(flat_hi, spread_lo[...], preferred_element_type=jnp.float32)
    )
    out_ref[...] = head + interact

    for step in steps:
        send_x(step).wait_send()
        for n in range(chunks):
            send_w(n, step).wait_send()
    for n in range(chunks):
        cross_copy(n).wait_send()
        final_copy(n).wait_send()
    for step in range(1, towers):
        send_o(step).wait_send()


def on_device(ids, tables, order, w_first, w_second, w_head, w_interact):
    towers = lax.axis_size("tower")
    devices = lax.axis_size("dev")
    samples, bag = ids.shape[2:]
    active, emb = tables.shape[2:]
    hidden = w_first.shape[2]
    zwidth = w_second.shape[2]
    heads = w_head.shape[1]
    block = samples // devices
    share = block // towers
    quarter = samples // RING
    pairs = w_interact.shape[0]
    tile = hidden // CHUNKS
    vmem = pltpu.VMEM
    dma = pltpu.SemaphoreType.DMA
    anywhere = pl.BlockSpec(memory_space=pl.ANY)
    scores = pl.pallas_call(
        functools.partial(kernel, towers=towers),
        out_shape=jax.ShapeDtypeStruct((share, heads), jnp.float32),
        in_specs=[
            anywhere,
            anywhere,
            pl.BlockSpec(memory_space=pltpu.SMEM),
            anywhere,
            anywhere,
            anywhere,
            anywhere,
        ],
        out_specs=pl.BlockSpec(memory_space=vmem),
        scratch_shapes=[
            vmem((bag, samples), jnp.int32),
            vmem((active, emb), jnp.bfloat16),
            vmem((samples, emb), jnp.float32),
            vmem((block, emb), jnp.float32),
            vmem((RING, quarter, emb), jnp.bfloat16),
            vmem((quarter, RING * emb), jnp.bfloat16),
            vmem((CHUNKS, RING * emb, tile), jnp.bfloat16),
            vmem((CHUNKS, CORES, 2, block, tile), jnp.float32),
            vmem((CHUNKS, 2, block, tile), jnp.float32),
            vmem((CHUNKS, block, tile), jnp.float32),
            vmem((CHUNKS, block, tile), jnp.float32),
            vmem((block, zwidth), jnp.float32),
            vmem((hidden, zwidth), jnp.bfloat16),
            vmem((towers, share, zwidth), jnp.bfloat16),
            vmem((towers, share, zwidth), jnp.bfloat16),
            vmem((towers, zwidth, heads), jnp.bfloat16),
            vmem((pairs, heads), jnp.float32),
            vmem((pairs * share, heads), jnp.bfloat16),
            vmem((pairs * share, heads), jnp.bfloat16),
            dma((5,)),
            dma((CHUNKS,)),
            dma((CHUNKS, RING)),
            dma((CHUNKS, RING)),
            dma((RING,)),
            dma((RING,)),
            dma((CHUNKS,)),
            dma((CHUNKS,)),
            dma((CHUNKS,)),
            dma((CHUNKS,)),
            dma((towers,)),
            dma((towers,)),
        ],
        compiler_params=pltpu.CompilerParams(
            collective_id=0, has_side_effects=True, vmem_limit_bytes=63 * 1024 * 1024
        ),
    )(
        jnp.swapaxes(ids[0, 0], 0, 1),
        tables[0, 0],
        order,
        w_first[0],
        w_second[0],
        w_head.reshape(towers, zwidth, heads),
        w_interact,
    )
    return scores[None]


def solution(mesh):
    return jax.shard_map(
        on_device,
        mesh=mesh,
        in_specs=(
            P("tower", "dev", None, None),
            P("tower", "dev", None, None),
            P(),
            P("tower", "dev", None),
            P("tower", None, None),
            P(),
            P(),
        ),
        out_specs=P("dev", "tower", None),
        check_vma=False,
    )
```

time: 68.2 us -> 56.5 us (0.83)
  local copies, waits for them, and re-layouts: 7.81 us -> 1.28 us
  Pallas kernels: 60.1 us -> 55.1 us
    unnamed x15 -> x1, local copies, waits for them, and re-layouts: 7.81 us -> 1.28 us
    pallas_call x1, Pallas kernels: 60.1 us -> 55.1 us  [on_device(): pl.pallas_call(functools.partial(kernel, towers=towers), out_shape=jax.Sh...]
where the time goes in v2:
time: 56.5 us; the launch traced here: 56.4 us
  Pallas kernels  55.1 us (98%)
  local copies, waits for them, and re-layouts  1.28 us (2%)
    pallas_call x1, Pallas kernels, on_device(): pl.pallas_call(functools.partial(kernel, towers=towers), out_shape=jax.Sh...  55.1 us
    unnamed x1, local copies, waits for them, and re-layouts  1.28 us

profile of v2, /device:TPU:1, one launch (start us, length us, event | category | flops | bytes accessed | tf_op | source)
XLA Modules:
  0.0 56.4 jit_solution(4955740708044208482)
XLA Ops:
  0.0 55.1 %shard_map.73 = f32[8,128]{1,0:T(8,128)} custom-call(s32[32,2048]{1,0:T(8,128)} %bitcast.10, bf16[512,128]{1,0:T(8,128)(2,1)} %bitcast.12, s32[2048]{0:T(1024)} %order_ref.1, bf16[128,1024]{1,0:T(8,128)(2,1)} %bitcast.11, bf16[1024,512]{1,0:T(8,128)(2,1)} %bitcast.9, bf16[16,512,128]{2,1,0:T(8,128)(2,1)} %bitcast.8, f32[256,128]{1,0:T(8,128)} %inter_hbm.1), custom_call_target="tpu_custom_call" | custom-call | tf_op jit(solution)/shard_map/pallas_call | solution.py:385
  55.1 1.3 %copy.9 = f32[1,8,128]{2,1,0:T(8,128)} copy(f32[1,8,128]{2,1,0:T(8,128)} %bitcast.13) | data formatting | bytes 8192

commit v3 on v2

--- a/solution.py
+++ b/solution.py
@@ -12,23 +12,57 @@
 RING = 4
 CORES = 2
 CHUNKS = 4
+EARLY = 2
+
+
+def fold(words, shift, mask):
+    return words & mask, lax.shift_right_logical(words, shift) & mask
+
+
+def tally(ids_ref, start, places):
+    bag = ids_ref.shape[0]
+    lanes = places.shape[1]
+    low_bits = places.shape[0]
+    shift = low_bits.bit_length() - 1
+    rows = [ids_ref[pl.ds(8 * g, 8), pl.ds(start, lanes)] for g in range(bag // 8)]
+    lows = [row & (low_bits - 1) for row in rows]
+    units = [jnp.left_shift(1, (row >> shift) << 1) for row in rows]
+
+    def mark(j):
+        low = lows[j // 8][j % 8 : j % 8 + 1, :]
+        unit = units[j // 8][j % 8 : j % 8 + 1, :]
+        return jnp.where(low == places, unit, 0)
+
+    def add(left, right):
+        return right if left is None else [a + b for a, b in zip(left, right)]
+
+    nibbles = None
+    bytes_ = None
+    held = 0
+    for start_j in range(0, bag, 3):
+        group = range(start_j, min(start_j + 3, bag))
+        words = mark(group[0])
+        for j in group[1:]:
+            words = words + mark(j)
+        nibbles = add(nibbles, fold(words, 2, 0x33333333))
+        held += len(group)
+        if held > 12 or group[-1] == bag - 1:
+            even = fold(nibbles[0], 4, 0x0F0F0F0F)
+            odd = fold(nibbles[1], 4, 0x0F0F0F0F)
+            bytes_ = add(bytes_, [even[0], odd[0], even[1], odd[1]])
+            nibbles = None
+            held = 0
+    return jnp.concatenate(bytes_, axis=0)
 
 
 def pool(ids_ref, table_ref, pooled_ref):
-    bag, samples = ids_ref.shape
+    samples = ids_ref.shape[1]
     active = table_ref.shape[0]
     lanes = 128
     fields = active // lanes
-    places = lax.broadcasted_iota(jnp.int32, (lanes, lanes), 0)
-
-    def chunk(index, carry):
-        start = pl.multiple_of(index * lanes, lanes)
-        packed = jnp.zeros((lanes, lanes), jnp.int32)
-        for j in range(bag):
-            row = ids_ref[pl.ds(j, 1), pl.ds(start, lanes)]
-            low = row & (lanes - 1)
-            unit = jnp.left_shift(1, (row >> 7) << 3)
-            packed = packed + jnp.where(low == places, unit, 0)
+    places = lax.broadcasted_iota(jnp.int32, (lanes // 4, lanes), 0)
+
+    def finish(packed, index):
         turned = packed.T
         counts = jnp.concatenate(
             [
@@ -37,12 +71,17 @@
             ],
             axis=1,
         )
-        pooled_ref[pl.ds(start, lanes), :] = jnp.dot(
+        pooled_ref[pl.ds(pl.multiple_of(index * lanes, lanes), lanes), :] = jnp.dot(
             counts, table_ref[...], preferred_element_type=jnp.float32
         )
-        return carry
-
-    lax.fori_loop(0, samples // lanes, chunk, 0)
+
+    def chunk(index, packed):
+        finish(packed, index - 1)
+        return tally(ids_ref, pl.multiple_of(index * lanes, lanes), places)
+
+    chunks = samples // lanes
+    last = lax.fori_loop(1, chunks, chunk, tally(ids_ref, 0, places))
+    finish(last, chunks - 1)
 
 
 def kernel(
@@ -137,9 +176,6 @@
     pl.semaphore_signal(barrier, inc=1, device_id=partner, device_id_type=MESH)
     pl.semaphore_signal(barrier, inc=1, device_id=across, device_id_type=MESH)
 
-    loads[0].wait()
-    loads[1].wait()
-    pool(ids_v, table_v, pooled)
     for copy in firsts:
         copy.wait()
     pl.semaphore_wait(barrier, towers - 1 + RING - 1 + 2)
@@ -180,8 +216,12 @@
                 lax.fori_loop(0, block // 16, group, 0)
                 store(c * 2 + x, permuted[...].astype(jnp.bfloat16))
 
-    for step in steps:
-        send_w(0, step).start()
+    for n in range(EARLY):
+        for step in steps:
+            send_w(n, step).start()
+    loads[0].wait()
+    loads[1].wait()
+    pool(ids_v, table_v, pooled)
     for step in steps:
         place = along(step)
 
@@ -190,7 +230,7 @@
 
         permute_rows(place, keep)
         send_x(step).start()
-    for n in range(1, chunks):
+    for n in range(EARLY, chunks):
         for step in steps:
             send_w(n, step).start()
 
@@ -381,7 +421,7 @@
     tile = hidden // CHUNKS
     vmem = pltpu.VMEM
     dma = pltpu.SemaphoreType.DMA
-    anywhere = pl.BlockSpec(memory_space=pl.ANY)
+    anywhere = pl.BlockSpec(memory_space=pltpu.HBM)
     scores = pl.pallas_call(
         functools.partial(kernel, towers=towers),
         out_shape=jax.ShapeDtypeStruct((share, heads), jnp.float32),
@@ -429,16 +469,21 @@
             dma((towers,)),
         ],
         compiler_params=pltpu.CompilerParams(
-            collective_id=0, has_side_effects=True, vmem_limit_bytes=63 * 1024 * 1024
+            collective_id=0, has_side_effects=True, vmem_limit_bytes=32 * 1024 * 1024
         ),
     )(
-        jnp.swapaxes(ids[0, 0], 0, 1),
-        tables[0, 0],
-        order,
-        w_first[0],
-        w_second[0],
-        w_head.reshape(towers, zwidth, heads),
-        w_interact,
+        *(
+            pltpu.with_memory_space_constraint(value, pltpu.HBM)
+            for value in (
+                jnp.swapaxes(ids[0, 0], 0, 1),
+                tables[0, 0],
+                order,
+                w_first[0],
+                w_second[0],
+                w_head.reshape(towers, zwidth, heads),
+                w_interact,
+            )
+        ),
     )
     return scores[None]
 

time: 56.5 us -> 50 us (0.88)
  Pallas kernels: 55.1 us -> 49.3 us
  local copies, waits for them, and re-layouts: 1.28 us -> 0.6 us
    pallas_call x1, Pallas kernels: 55.1 us -> 49.3 us  [on_device(): pl.pallas_call(functools.partial(kernel, towers=towers), out_shape=jax.Sh...]
    unnamed x1, local copies, waits for them, and re-layouts: 1.28 us -> 0.6 us
where the time goes in v3:
time: 50 us; the launch traced here: 49.9 us
  Pallas kernels  49.3 us (99%)
  local copies, waits for them, and re-layouts  0.6 us (1%)
    pallas_call x1, Pallas kernels, on_device(): pl.pallas_call(functools.partial(kernel, towers=towers), out_shape=jax.Sh...  49.3 us

profile of v3, /device:TPU:1, one launch (start us, length us, event | category | flops | bytes accessed | tf_op | source)
XLA Modules:
  0.0 49.9 jit_solution(8553456074288284045)
XLA Ops:
  0.0 49.3 %shard_map.73 = f32[8,128]{1,0:T(8,128)S(1)} custom-call(s32[32,2048]{1,0:T(8,128)} %bitcast.11, bf16[512,128]{1,0:T(8,128)(2,1)} %bitcast.13, s32[2048]{0:T(1024)} %order_ref.1, bf16[128,1024]{1,0:T(8,128)(2,1)} %bitcast.12, bf16[1024,512]{1,0:T(8,128)(2,1)} %bitcast.10, bf16[16,512,128]{2,1,0:T(8,128)(2,1)} %bitcast.9, f32[256,128]{1,0:T(8,128)} %inter_hbm.1), custom_call_target="tpu_custom_call" | custom-call | tf_op jit(solution)/shard_map/pallas_call | solution.py:425
  49.3 0.6 %copy.9 = f32[1,8,128]{2,1,0:T(8,128)} copy(f32[1,8,128]{2,1,0:T(8,128)S(1)} %bitcast.8) | data formatting | bytes 8192

commit v4 on v3

--- a/solution.py
+++ b/solution.py
@@ -13,6 +13,7 @@
 CORES = 2
 CHUNKS = 4
 EARLY = 2
+LEVELS = 32767
 
 
 def fold(words, shift, mask):
@@ -104,6 +105,8 @@
     cross,
     relay,
     final,
+    relay_top,
+    final_top,
     outsum,
     second_v,
     outbox,
@@ -293,15 +296,18 @@
             device_id_type=MESH,
         )
 
-    def final_copy(n):
-        return pltpu.make_async_remote_copy(
-            src_ref=relay.at[n],
-            dst_ref=final.at[n],
-            send_sem=f_send.at[n],
-            recv_sem=f_recv.at[n],
-            device_id=across,
-            device_id_type=MESH,
-        )
+    def final_copies(n):
+        return [
+            pltpu.make_async_remote_copy(
+                src_ref=source.at[n],
+                dst_ref=target.at[n],
+                send_sem=f_send.at[n, which],
+                recv_sem=f_recv.at[n, which],
+                device_id=across,
+                device_id_type=MESH,
+            )
+            for which, (source, target) in enumerate(((relay_top, final_top), (relay, final)))
+        ]
 
     def first_layer(n):
         if n == 0:
@@ -315,12 +321,19 @@
 
     def add_cores(n):
         cross_copy(n).wait_recv()
-        relay[n] = total[n, core, 1 - col] + cross[n, 1 - col]
-        final_copy(n).start()
+        part = total[n, core, 1 - col] + cross[n, 1 - col]
+        top = jnp.max(jnp.abs(part), axis=0, keepdims=True)
+        steps_up = part * (LEVELS / jnp.maximum(top, 1e-30)) + (LEVELS + 1.5)
+        relay[n] = (steps_up.astype(jnp.int32) - (LEVELS + 1)).astype(jnp.int16)
+        relay_top[n] = jnp.broadcast_to(top, relay_top.shape[1:])
+        for copy in final_copies(n):
+            copy.start()
 
     def second_layer(n):
-        final_copy(n).wait_recv()
-        preact = total[n, core, col] + cross[n, col] + final[n]
+        for copy in final_copies(n):
+            copy.wait_recv()
+        other = final[n].astype(jnp.float32) * (final_top[n, 0:1, :] * (1.0 / LEVELS))
+        preact = total[n, core, col] + cross[n, col] + other
         hidden = jnp.maximum(preact, 0.0).astype(jnp.bfloat16)
         part = jnp.dot(
             hidden, second_v[n * tile : (n + 1) * tile, :], preferred_element_type=jnp.float32
@@ -401,7 +414,8 @@
             send_w(n, step).wait_send()
     for n in range(chunks):
         cross_copy(n).wait_send()
-        final_copy(n).wait_send()
+        for copy in final_copies(n):
+            copy.wait_send()
     for step in range(1, towers):
         send_o(step).wait_send()
 
@@ -445,8 +459,10 @@
             vmem((CHUNKS, RING * emb, tile), jnp.bfloat16),
             vmem((CHUNKS, CORES, 2, block, tile), jnp.float32),
             vmem((CHUNKS, 2, block, tile), jnp.float32),
-            vmem((CHUNKS, block, tile), jnp.float32),
-            vmem((CHUNKS, block, tile), jnp.float32),
+            vmem((CHUNKS, block, tile), jnp.int16),
+            vmem((CHUNKS, block, tile), jnp.int16),
+            vmem((CHUNKS, 8, tile), jnp.float32),
+            vmem((CHUNKS, 8, tile), jnp.float32),
             vmem((block, zwidth), jnp.float32),
             vmem((hidden, zwidth), jnp.bfloat16),
             vmem((towers, share, zwidth), jnp.bfloat16),
@@ -463,8 +479,8 @@
             dma((RING,)),
             dma((CHUNKS,)),
             dma((CHUNKS,)),
-            dma((CHUNKS,)),
-            dma((CHUNKS,)),
+            dma((CHUNKS, 2)),
+            dma((CHUNKS, 2)),
             dma((towers,)),
             dma((towers,)),
         ],

time: 50 us -> 45.5 us (0.910)
  Pallas kernels: 49.3 us -> 44.8 us
    pallas_call x1, Pallas kernels: 49.3 us -> 44.8 us  [on_device(): pl.pallas_call(functools.partial(kernel, towers=towers), out_shape=jax.Sh...]
where the time goes in v4:
time: 45.5 us; the launch traced here: 45.4 us
  Pallas kernels  44.8 us (98%)
  local copies, waits for them, and re-layouts  0.6 us (1%)
    pallas_call x1, Pallas kernels, on_device(): pl.pallas_call(functools.partial(kernel, towers=towers), out_shape=jax.Sh...  44.8 us

profile of v4, /device:TPU:1, one launch (start us, length us, event | category | flops | bytes accessed | tf_op | source)
XLA Modules:
  0.0 45.4 jit_solution(7722216130417517907)
XLA Ops:
  0.0 44.8 %shard_map.73 = f32[8,128]{1,0:T(8,128)S(1)} custom-call(s32[32,2048]{1,0:T(8,128)} %bitcast.11, bf16[512,128]{1,0:T(8,128)(2,1)} %bitcast.13, s32[2048]{0:T(1024)} %order_ref.1, bf16[128,1024]{1,0:T(8,128)(2,1)} %bitcast.12, bf16[1024,512]{1,0:T(8,128)(2,1)} %bitcast.10, bf16[16,512,128]{2,1,0:T(8,128)(2,1)} %bitcast.9, f32[256,128]{1,0:T(8,128)} %inter_hbm.1), custom_call_target="tpu_custom_call" | custom-call | tf_op jit(solution)/shard_map/pallas_call | solution.py:439
  44.8 0.6 %copy.9 = f32[1,8,128]{2,1,0:T(8,128)} copy(f32[1,8,128]{2,1,0:T(8,128)S(1)} %bitcast.8) | data formatting | bytes 8192

commit v5 on v4

--- a/solution.py
+++ b/solution.py
@@ -12,8 +12,26 @@
 RING = 4
 CORES = 2
 CHUNKS = 4
-EARLY = 2
+SPANS = ((0, 2), (2, 1), (3, 1))
+EARLY = 1
 LEVELS = 32767
+HOPS = (
+    (1, 0),
+    (7, 0),
+    (2, 0),
+    (6, 0),
+    (0, 1),
+    (1, 1),
+    (7, 1),
+    (3, 0),
+    (5, 0),
+    (2, 1),
+    (6, 1),
+    (4, 0),
+    (3, 1),
+    (5, 1),
+    (4, 1),
+)
 
 
 def fold(words, shift, mask):
@@ -127,6 +145,9 @@
     f_recv,
     o_send,
     o_recv,
+    near_sem,
+    far_sem,
+    open_sem,
     towers,
 ):
     tower = lax.axis_index("tower")
@@ -170,25 +191,64 @@
         copy.start()
 
     barrier = pltpu.get_barrier_semaphore()
-    for step in range(1, towers):
-        pl.semaphore_signal(
-            barrier, inc=1, device_id={"tower": lax.rem(tower + step, towers)}, device_id_type=MESH
-        )
-    for step in range(1, RING):
-        pl.semaphore_signal(barrier, inc=1, device_id=at_row(along(step)), device_id_type=MESH)
-    pl.semaphore_signal(barrier, inc=1, device_id=partner, device_id_type=MESH)
-    pl.semaphore_signal(barrier, inc=1, device_id=across, device_id_type=MESH)
+    devices = CORES * RING * 2
+    gate = dev == 0
+    peers = [at_row(along(step))["dev"] for step in range(1, RING)]
+    peers += [partner["dev"], across["dev"]]
+    near = jnp.int32(0)
+    for peer in peers:
+        near = near + jnp.where(peer == 0, 1, 0)
+
+    @pl.when(jnp.logical_not(gate))
+    def _():
+        for peer in peers:
+
+            @pl.when(peer != 0)
+            def _():
+                pl.semaphore_signal(
+                    barrier, inc=1, device_id={"dev": peer}, device_id_type=MESH
+                )
+
+        pl.semaphore_wait(barrier, len(peers) + 1 - near)
+
+        @pl.when(near == 1)
+        def _():
+            pl.semaphore_signal(near_sem, inc=1, device_id={"dev": 0}, device_id_type=MESH)
+
+        @pl.when(near == 0)
+        def _():
+            pl.semaphore_signal(far_sem, inc=1, device_id={"dev": 0}, device_id_type=MESH)
+
+    @pl.when(gate)
+    def _():
+        for other in range(1, devices):
+            pl.semaphore_signal(barrier, inc=1, device_id={"dev": other}, device_id_type=MESH)
+        pl.semaphore_wait(near_sem, len(peers))
+
+    def gate_towers():
+        pl.semaphore_wait(far_sem, devices - 1 - len(peers))
+        for step in range(1, towers):
+            pl.semaphore_signal(
+                barrier,
+                inc=1,
+                device_id={"tower": lax.rem(tower + step, towers)},
+                device_id_type=MESH,
+            )
+
+    def gate_open():
+        pl.semaphore_wait(barrier, towers - 1)
+        for other in range(1, devices):
+            pl.semaphore_signal(open_sem, inc=1, device_id={"dev": other}, device_id_type=MESH)
 
     for copy in firsts:
         copy.wait()
-    pl.semaphore_wait(barrier, towers - 1 + RING - 1 + 2)
 
     steps = (1, 3, 2)
 
     def send_w(n, step):
         return pltpu.make_async_remote_copy(
-            src_ref=wall.at[n, mine, :],
-            dst_ref=wall.at[n, mine, :],
+            src_ref=wall.at[pl.ds(*SPANS[n]), mine, :],
+            dst_ref=wall.at[pl.ds(*SPANS[n]), mine, :],
             send_sem=w_send.at[n, step],
             recv_sem=w_recv.at[n, row],
             device_id=at_row(along(step)),
@@ -222,6 +282,7 @@
     for n in range(EARLY):
         for step in steps:
             send_w(n, step).start()
+    pl.when(gate)(gate_towers)
     loads[0].wait()
     loads[1].wait()
     pool(ids_v, table_v, pooled)
@@ -233,7 +294,7 @@
 
         permute_rows(place, keep)
         send_x(step).start()
-    for n in range(EARLY, chunks):
+    for n in range(EARLY, len(SPANS)):
         for step in steps:
             send_w(n, step).start()
 
@@ -241,6 +302,7 @@
         xall[part * block : (part + 1) * block, mine] = value
 
     permute_rows(row, keep_own)
+    pl.when(gate)(gate_open)
 
     loads[4].wait()
     pairs = inter_v.shape[0]
@@ -266,8 +328,8 @@
         source = along(step)
         span = pl.ds(pl.multiple_of(source * emb, emb), emb)
         return pltpu.make_async_remote_copy(
-            src_ref=wall.at[n, span, :],
-            dst_ref=wall.at[n, span, :],
+            src_ref=wall.at[pl.ds(*SPANS[n]), span, :],
+            dst_ref=wall.at[pl.ds(*SPANS[n]), span, :],
             send_sem=w_send.at[n, step],
             recv_sem=w_recv.at[n, source],
             device_id=partner,
@@ -313,8 +375,10 @@
         if n == 0:
             for step in steps:
                 arrived_x(step).wait_recv()
-        for step in steps:
-            arrived_w(n, step).wait_recv()
+        for index, (begin, _) in enumerate(SPANS):
+            if begin == n:
+                for step in steps:
+                    arrived_w(index, step).wait_recv()
         part = jnp.dot(xall[...], wall[n], preferred_element_type=jnp.float32)
         total[n] = part.reshape(CORES, 2, block, tile)
         cross_copy(n).start()
@@ -354,37 +418,45 @@
     share = outbox.shape[1]
     outbox[...] = outsum[...].reshape(towers, share, outsum.shape[1]).astype(jnp.bfloat16)
 
-    def send_o(step):
-        peer = lax.rem(tower + step, towers)
+    depth = towers // 2
+
+    def other_tower(dz, dx):
+        return lax.rem(tower // 2 + dz, depth) * 2 + lax.rem(lax.rem(tower, 2) + dx, 2)
+
+    def send_o(dz, dx):
+        peer = other_tower(dz, dx)
         return pltpu.make_async_remote_copy(
             src_ref=outbox.at[peer],
             dst_ref=inbox.at[tower],
-            send_sem=o_send.at[step],
+            send_sem=o_send.at[dz * 2 + dx],
             recv_sem=o_recv.at[tower],
             device_id={"tower": peer},
             device_id_type=MESH,
         )
 
-    for step in range(1, towers):
-        send_o(step).start()
+    @pl.when(jnp.logical_not(gate))
+    def _():
+        pl.semaphore_wait(open_sem, 1)
+
+    for dz, dx in reversed(HOPS):
+        send_o(dz, dx).start()
     inbox[tower] = outbox[tower]
 
     def head_part(source):
         return jnp.dot(inbox[source], head_v[source], preferred_element_type=jnp.float32)
 
-    def collect(step, value):
-        source = lax.rem(tower + towers - step, towers)
+    head = head_part(tower)
+    for dz, dx in HOPS:
+        source = other_tower(dz, dx)
         pltpu.make_async_remote_copy(
             src_ref=outbox.at[source],
             dst_ref=inbox.at[source],
-            send_sem=o_send.at[step],
+            send_sem=o_send.at[dz * 2 + dx],
             recv_sem=o_recv.at[source],
             device_id=partner,
             device_id_type=MESH,
         ).wait_recv()
-        return value + head_part(source)
-
-    head = lax.fori_loop(1, towers, collect, head_part(tower))
+        head = head + head_part(source)
 
     zwidth = inbox.shape[2]
     stacked = (
@@ -400,24 +472,23 @@
         [gram[t * share : (t + 1) * share, :] for t in range(towers)], axis=1
     )
     flat_hi = flat.astype(jnp.bfloat16)
-    flat_lo = (flat - flat_hi.astype(jnp.float32)).astype(jnp.bfloat16)
-    interact = (
-        jnp.dot(flat_hi, spread_hi[...], preferred_element_type=jnp.float32)
-        + jnp.dot(flat_lo, spread_hi[...], preferred_element_type=jnp.float32)
-        + jnp.dot(flat_hi, spread_lo[...], preferred_element_type=jnp.float32)
-    )
+    rest = flat - flat_hi.astype(jnp.float32)
+    both = jnp.concatenate([flat_hi.astype(jnp.float32), rest], axis=0).astype(jnp.bfloat16)
+    twice = jnp.dot(both, spread_hi[...], preferred_element_type=jnp.float32)
+    interact = twice[:share] + twice[share:]
+    interact += jnp.dot(flat_hi, spread_lo[...], preferred_element_type=jnp.float32)
     out_ref[...] = head + interact
 
     for step in steps:
         send_x(step).wait_send()
-        for n in range(chunks):
+        for n in range(len(SPANS)):
             send_w(n, step).wait_send()
     for n in range(chunks):
         cross_copy(n).wait_send()
         for copy in final_copies(n):
             copy.wait_send()
-    for step in range(1, towers):
-        send_o(step).wait_send()
+    for dz, dx in HOPS:
+        send_o(dz, dx).wait_send()
 
 
 def on_device(ids, tables, order, w_first, w_second, w_head, w_interact):
@@ -473,8 +544,8 @@
             vmem((pairs * share, heads), jnp.bfloat16),
             dma((5,)),
             dma((CHUNKS,)),
-            dma((CHUNKS, RING)),
-            dma((CHUNKS, RING)),
+            dma((len(SPANS), RING)),
+            dma((len(SPANS), RING)),
             dma((RING,)),
             dma((RING,)),
             dma((CHUNKS,)),
@@ -483,6 +554,9 @@
             dma((CHUNKS, 2)),
             dma((towers,)),
             dma((towers,)),
+            pltpu.SemaphoreType.REGULAR,
+            pltpu.SemaphoreType.REGULAR,
+            pltpu.SemaphoreType.REGULAR,
         ],
         compiler_params=pltpu.CompilerParams(
             collective_id=0, has_side_effects=True, vmem_limit_bytes=32 * 1024 * 1024

time: 45.5 us -> 45.2 us (level)
  the two profiles are of different devices: /device:TPU:1 before, /device:TPU:24 now
where the time goes in v5:
time: 45.2 us; the launch traced here: 45.1 us
  Pallas kernels  44.5 us (98%)
  local copies, waits for them, and re-layouts  0.6 us (1%)
    pallas_call x1, Pallas kernels, on_device(): pl.pallas_call(functools.partial(kernel, towers=towers), out_shape=jax.Sh...  44.5 us

profile of v5, /device:TPU:24, one launch (start us, length us, event | category | flops | bytes accessed | tf_op | source)
XLA Modules:
  0.0 45.1 jit_solution(1993712815407855100)
XLA Ops:
  0.0 44.5 %shard_map.73 = f32[8,128]{1,0:T(8,128)S(1)} custom-call(s32[32,2048]{1,0:T(8,128)} %bitcast.11, bf16[512,128]{1,0:T(8,128)(2,1)} %bitcast.13, s32[2048]{0:T(1024)} %order_ref.1, bf16[128,1024]{1,0:T(8,128)(2,1)} %bitcast.12, bf16[1024,512]{1,0:T(8,128)(2,1)} %bitcast.10, bf16[16,512,128]{2,1,0:T(8,128)(2,1)} %bitcast.9, f32[256,128]{1,0:T(8,128)} %inter_hbm.1), custom_call_target="tpu_custom_call" | custom-call | tf_op jit(solution)/shard_map/pallas_call | solution.py:510
  44.5 0.6 %copy.9 = f32[1,8,128]{2,1,0:T(8,128)} copy(f32[1,8,128]{2,1,0:T(8,128)S(1)} %bitcast.8) | data formatting | bytes 8192

commit v6 on v5

--- a/solution.py
+++ b/solution.py
@@ -11,9 +11,11 @@
 MESH = pl.DeviceIdType.MESH
 RING = 4
 CORES = 2
-CHUNKS = 4
-SPANS = ((0, 2), (2, 1), (3, 1))
+CHUNKS = 8
+SPANS = ((0, 4), (4, 2), (6, 2))
+GROUPS = ((0, 2), (2, 2), (4, 2), (6, 2))
 EARLY = 1
+RELAYED = 0
 LEVELS = 32767
 HOPS = (
     (1, 0),
@@ -137,6 +139,8 @@
     first_sem,
     w_send,
     w_recv,
+    r_send,
+    r_recv,
     x_send,
     x_recv,
     c_send,
@@ -255,53 +259,115 @@
             device_id_type=MESH,
         )
 
-    def send_x(step):
-        return pltpu.make_async_remote_copy(
-            src_ref=xsend.at[along(step)],
-            dst_ref=xall.at[:, mine],
-            send_sem=x_send.at[step],
-            recv_sem=x_recv.at[row],
+    def forward(n, half):
+        source = along(3) if half == 0 else along(1)
+        span = pl.ds(pl.multiple_of(source * emb + half * (emb // 2), emb // 2), emb // 2)
+        return pltpu.make_async_remote_copy(
+            src_ref=wall.at[pl.ds(*SPANS[n]), span, :],
+            dst_ref=wall.at[pl.ds(*SPANS[n]), span, :],
+            send_sem=r_send.at[n, half],
+            recv_sem=r_recv.at[n, half],
+            device_id=at_row(along(1) if half == 0 else along(3)),
+            device_id_type=MESH,
+        )
+
+    def forwarded(n, half):
+        source = along(2)
+        span = pl.ds(pl.multiple_of(source * emb + half * (emb // 2), emb // 2), emb // 2)
+        return pltpu.make_async_remote_copy(
+            src_ref=wall.at[pl.ds(*SPANS[n]), span, :],
+            dst_ref=wall.at[pl.ds(*SPANS[n]), span, :],
+            send_sem=r_send.at[n, half],
+            recv_sem=r_recv.at[n, half],
+            device_id=partner,
+            device_id_type=MESH,
+        )
+
+    def w_steps(n):
+        return steps[:2] if n < RELAYED else steps
+
+    def arrived_w(n, step):
+        source = along(step)
+        span = pl.ds(pl.multiple_of(source * emb, emb), emb)
+        return pltpu.make_async_remote_copy(
+            src_ref=wall.at[pl.ds(*SPANS[n]), span, :],
+            dst_ref=wall.at[pl.ds(*SPANS[n]), span, :],
+            send_sem=w_send.at[n, step],
+            recv_sem=w_recv.at[n, source],
+            device_id=partner,
+            device_id_type=MESH,
+        )
+
+    def send_x(kind, step):
+        return pltpu.make_async_remote_copy(
+            src_ref=xsend.at[kind, along(step)],
+            dst_ref=xall.at[kind, :, mine],
+            send_sem=x_send.at[kind, step],
+            recv_sem=x_recv.at[kind, row],
             device_id=at_row(along(step)),
             device_id_type=MESH,
         )
 
-    def permute_rows(place, store):
+    def arrived_x(kind, step):
+        source = along(step)
+        span = pl.ds(pl.multiple_of(source * emb, emb), emb)
+        return pltpu.make_async_remote_copy(
+            src_ref=xsend.at[kind, source],
+            dst_ref=xall.at[kind, :, span],
+            send_sem=x_send.at[kind, step],
+            recv_sem=x_recv.at[kind, source],
+            device_id=partner,
+            device_id_type=MESH,
+        )
+
+    def permute_rows(kind, place, store):
+        x = 1 - col if kind == 0 else col
         for c in range(CORES):
-            for x in range(2):
-                start = ((x * RING + place) * CORES + c) * block
-
-                def group(index, carry):
-                    for q in range(16):
-                        source = order_ref[start + index * 16 + q]
-                        permuted[pl.ds(index * 16 + q, 1), :] = pooled[pl.ds(source, 1), :]
-                    return carry
-
-                lax.fori_loop(0, block // 16, group, 0)
-                store(c * 2 + x, permuted[...].astype(jnp.bfloat16))
+            start = ((x * RING + place) * CORES + c) * block
+
+            def group(index, carry):
+                for q in range(16):
+                    source = order_ref[start + index * 16 + q]
+                    permuted[pl.ds(index * 16 + q, 1), :] = pooled[pl.ds(source, 1), :]
+                return carry
+
+            lax.fori_loop(0, block // 16, group, 0)
+            store(c, permuted[...].astype(jnp.bfloat16))
+
+    def permute_send(kind):
+        for step in steps:
+            place = along(step)
+
+            def keep(part, value):
+                xsend[kind, place, part * block : (part + 1) * block, :] = value
+
+            permute_rows(kind, place, keep)
+            send_x(kind, step).start()
+
+    def permute_own(kind):
+        def keep(part, value):
+            xall[kind, part * block : (part + 1) * block, mine] = value
+
+        permute_rows(kind, row, keep)
 
     for n in range(EARLY):
-        for step in steps:
+        for step in w_steps(n):
             send_w(n, step).start()
     pl.when(gate)(gate_towers)
     loads[0].wait()
     loads[1].wait()
     pool(ids_v, table_v, pooled)
-    for step in steps:
-        place = along(step)
-
-        def keep(part, value):
-            xsend[place, part * block : (part + 1) * block, :] = value
-
-        permute_rows(place, keep)
-        send_x(step).start()
+    permute_send(0)
+    for n in range(RELAYED):
+        for half, near_step in ((0, 3), (1, 1)):
+            arrived_w(n, near_step).wait_recv()
+            forward(n, half).start()
     for n in range(EARLY, len(SPANS)):
-        for step in steps:
+        for step in w_steps(n):
             send_w(n, step).start()
-
-    def keep_own(part, value):
-        xall[part * block : (part + 1) * block, mine] = value
-
-    permute_rows(row, keep_own)
+    permute_own(0)
+    permute_send(1)
+    permute_own(1)
     pl.when(gate)(gate_open)
 
     loads[4].wait()
@@ -324,96 +390,94 @@
     loads[2].wait()
     loads[3].wait()
 
-    def arrived_w(n, step):
-        source = along(step)
-        span = pl.ds(pl.multiple_of(source * emb, emb), emb)
-        return pltpu.make_async_remote_copy(
-            src_ref=wall.at[pl.ds(*SPANS[n]), span, :],
-            dst_ref=wall.at[pl.ds(*SPANS[n]), span, :],
-            send_sem=w_send.at[n, step],
-            recv_sem=w_recv.at[n, source],
+    def cross_copy(kind, g):
+        return pltpu.make_async_remote_copy(
+            src_ref=total.at[kind, pl.ds(*GROUPS[g]), 1 - core],
+            dst_ref=cross.at[kind, pl.ds(*GROUPS[g])],
+            send_sem=c_send.at[kind, g],
+            recv_sem=c_recv.at[kind, g],
             device_id=partner,
             device_id_type=MESH,
         )
 
-    def arrived_x(step):
-        source = along(step)
-        span = pl.ds(pl.multiple_of(source * emb, emb), emb)
-        return pltpu.make_async_remote_copy(
-            src_ref=xsend.at[source],
-            dst_ref=xall.at[:, span],
-            send_sem=x_send.at[step],
-            recv_sem=x_recv.at[source],
-            device_id=partner,
-            device_id_type=MESH,
-        )
-
-    def cross_copy(n):
-        return pltpu.make_async_remote_copy(
-            src_ref=total.at[n, 1 - core],
-            dst_ref=cross.at[n],
-            send_sem=c_send.at[n],
-            recv_sem=c_recv.at[n],
-            device_id=partner,
-            device_id_type=MESH,
-        )
-
-    def final_copies(n):
+    def final_copies(g):
         return [
             pltpu.make_async_remote_copy(
-                src_ref=source.at[n],
-                dst_ref=target.at[n],
-                send_sem=f_send.at[n, which],
-                recv_sem=f_recv.at[n, which],
+                src_ref=source.at[pl.ds(*GROUPS[g])],
+                dst_ref=target.at[pl.ds(*GROUPS[g])],
+                send_sem=f_send.at[g, which],
+                recv_sem=f_recv.at[g, which],
                 device_id=across,
                 device_id_type=MESH,
             )
             for which, (source, target) in enumerate(((relay_top, final_top), (relay, final)))
         ]
 
-    def first_layer(n):
-        if n == 0:
-            for step in steps:
-                arrived_x(step).wait_recv()
+    def tiles(g):
+        return range(GROUPS[g][0], sum(GROUPS[g]))
+
+    def arrived_span(g):
         for index, (begin, _) in enumerate(SPANS):
-            if begin == n:
-                for step in steps:
-                    arrived_w(index, step).wait_recv()
-        part = jnp.dot(xall[...], wall[n], preferred_element_type=jnp.float32)
-        total[n] = part.reshape(CORES, 2, block, tile)
-        cross_copy(n).start()
-
-    def add_cores(n):
-        cross_copy(n).wait_recv()
-        part = total[n, core, 1 - col] + cross[n, 1 - col]
-        top = jnp.max(jnp.abs(part), axis=0, keepdims=True)
-        steps_up = part * (LEVELS / jnp.maximum(top, 1e-30)) + (LEVELS + 1.5)
-        relay[n] = (steps_up.astype(jnp.int32) - (LEVELS + 1)).astype(jnp.int16)
-        relay_top[n] = jnp.broadcast_to(top, relay_top.shape[1:])
-        for copy in final_copies(n):
+            if begin in tiles(g):
+                if index < RELAYED:
+                    for half in range(2):
+                        forwarded(index, half).wait_recv()
+                else:
+                    for step in steps:
+                        arrived_w(index, step).wait_recv()
+
+    def first_layer(kind, g):
+        for n in tiles(g):
+            part = jnp.dot(xall[kind], wall[n], preferred_element_type=jnp.float32)
+            total[kind, n] = part.reshape(CORES, block, tile)
+        cross_copy(kind, g).start()
+
+    def add_cores(g):
+        cross_copy(0, g).wait_recv()
+        for n in tiles(g):
+            part = total[0, n, core] + cross[0, n]
+            top = jnp.max(jnp.abs(part), axis=0, keepdims=True)
+            steps_up = part * (LEVELS / jnp.maximum(top, 1e-30)) + (LEVELS + 1.5)
+            relay[n] = (steps_up.astype(jnp.int32) - (LEVELS + 1)).astype(jnp.int16)
+            relay_top[n] = jnp.broadcast_to(top, relay_top.shape[1:])
+        for copy in final_copies(g):
             copy.start()
 
-    def second_layer(n):
-        for copy in final_copies(n):
+    def second_layer(g):
+        cross_copy(1, g).wait_recv()
+        for copy in final_copies(g):
             copy.wait_recv()
-        other = final[n].astype(jnp.float32) * (final_top[n, 0:1, :] * (1.0 / LEVELS))
-        preact = total[n, core, col] + cross[n, col] + other
-        hidden = jnp.maximum(preact, 0.0).astype(jnp.bfloat16)
+        hidden = []
+        for n in tiles(g):
+            other = final[n].astype(jnp.float32) * (final_top[n, 0:1, :] * (1.0 / LEVELS))
+            preact = total[1, n, core] + cross[1, n] + other
+            hidden.append(jnp.maximum(preact, 0.0).astype(jnp.bfloat16))
+        begin, count = GROUPS[g]
         part = jnp.dot(
-            hidden, second_v[n * tile : (n + 1) * tile, :], preferred_element_type=jnp.float32
-        )
-        if n == 0:
+            jnp.concatenate(hidden, axis=1),
+            second_v[begin * tile : (begin + count) * tile, :],
+            preferred_element_type=jnp.float32,
+        )
+        if g == 0:
             outsum[...] = part
         else:
             outsum[...] += part
 
-    for n in range(chunks + 2):
-        if n < chunks:
-            first_layer(n)
-        if 1 <= n <= chunks:
-            add_cores(n - 1)
-        if n >= 2:
-            second_layer(n - 2)
+    groups = len(GROUPS)
+    for step in steps:
+        arrived_x(0, step).wait_recv()
+    for g in range(groups + 1):
+        if g < groups:
+            arrived_span(g)
+            first_layer(0, g)
+        if g >= 1:
+            add_cores(g - 1)
+    for step in steps:
+        arrived_x(1, step).wait_recv()
+    for g in range(groups):
+        first_layer(1, g)
+    for g in range(groups):
+        second_layer(g)
 
     share = outbox.shape[1]
     outbox[...] = outsum[...].reshape(towers, share, outsum.shape[1]).astype(jnp.bfloat16)
@@ -480,12 +544,18 @@
     out_ref[...] = head + interact
 
     for step in steps:
-        send_x(step).wait_send()
+        send_x(0, step).wait_send()
+        send_x(1, step).wait_send()
         for n in range(len(SPANS)):
-            send_w(n, step).wait_send()
-    for n in range(chunks):
-        cross_copy(n).wait_send()
-        for copy in final_copies(n):
+            if step in w_steps(n):
+                send_w(n, step).wait_send()
+    for n in range(RELAYED):
+        for half in range(2):
+            forward(n, half).wait_send()
+    for g in range(groups):
+        cross_copy(0, g).wait_send()
+        cross_copy(1, g).wait_send()
+        for copy in final_copies(g):
             copy.wait_send()
     for dz, dx in HOPS:
         send_o(dz, dx).wait_send()
@@ -525,11 +595,11 @@
             vmem((active, emb), jnp.bfloat16),
             vmem((samples, emb), jnp.float32),
             vmem((block, emb), jnp.float32),
-            vmem((RING, quarter, emb), jnp.bfloat16),
-            vmem((quarter, RING * emb), jnp.bfloat16),
+            vmem((2, RING, quarter // 2, emb), jnp.bfloat16),
+            vmem((2, quarter // 2, RING * emb), jnp.bfloat16),
             vmem((CHUNKS, RING * emb, tile), jnp.bfloat16),
-            vmem((CHUNKS, CORES, 2, block, tile), jnp.float32),
-            vmem((CHUNKS, 2, block, tile), jnp.float32),
+            vmem((2, CHUNKS, CORES, block, tile), jnp.float32),
+            vmem((2, CHUNKS, block, tile), jnp.float32),
             vmem((CHUNKS, block, tile), jnp.int16),
             vmem((CHUNKS, block, tile), jnp.int16),
             vmem((CHUNKS, 8, tile), jnp.float32),
@@ -546,10 +616,12 @@
             dma((CHUNKS,)),
             dma((len(SPANS), RING)),
             dma((len(SPANS), RING)),
-            dma((RING,)),
-            dma((RING,)),
-            dma((CHUNKS,)),
-            dma((CHUNKS,)),
+            dma((len(SPANS), 2)),
+            dma((len(SPANS), 2)),
+            dma((2, RING)),
+            dma((2, RING)),
+            dma((2, CHUNKS)),
+            dma((2, CHUNKS)),
             dma((CHUNKS, 2)),
             dma((CHUNKS, 2)),
             dma((towers,)),

time: 45.2 us -> 41.8 us (0.925)
  the two profiles are of different devices: /device:TPU:24 before, /device:TPU:1 now
where the time goes in v6:
time: 41.8 us; the launch traced here: 41.4 us
  Pallas kernels  40.8 us (98%)
  local copies, waits for them, and re-layouts  0.6 us (1%)
    pallas_call x1, Pallas kernels, on_device(): pl.pallas_call(functools.partial(kernel, towers=towers), out_shape=jax.Sh...  40.8 us

profile of v6, /device:TPU:1, one launch (start us, length us, event | category | flops | bytes accessed | tf_op | source)
XLA Modules:
  0.0 41.4 jit_solution(14611491467261609239)
XLA Ops:
  0.0 40.8 %shard_map.73 = f32[8,128]{1,0:T(8,128)S(1)} custom-call(s32[32,2048]{1,0:T(8,128)} %bitcast.11, bf16[512,128]{1,0:T(8,128)(2,1)} %bitcast.13, s32[2048]{0:T(1024)} %order_ref.1, bf16[128,1024]{1,0:T(8,128)(2,1)} %bitcast.12, bf16[1024,512]{1,0:T(8,128)(2,1)} %bitcast.10, bf16[16,512,128]{2,1,0:T(8,128)(2,1)} %bitcast.9, f32[256,128]{1,0:T(8,128)} %inter_hbm.1), custom_call_target="tpu_custom_call" | custom-call | tf_op jit(solution)/shard_map/pallas_call | solution.py:580
  40.8 0.6 %copy.9 = f32[1,8,128]{2,1,0:T(8,128)} copy(f32[1,8,128]{2,1,0:T(8,128)S(1)} %bitcast.8) | data formatting | bytes 8192

commit v7 on v6

--- a/solution.py
+++ b/solution.py
@@ -12,11 +12,15 @@
 RING = 4
 CORES = 2
 CHUNKS = 8
+BATCH = 8
+UNROLL = 1
 SPANS = ((0, 4), (4, 2), (6, 2))
 GROUPS = ((0, 2), (2, 2), (4, 2), (6, 2))
-EARLY = 1
-RELAYED = 0
-LEVELS = 32767
+EARLY = 2
+RELAYED = 2
+AHEAD = 0
+LEVELS = 32752
+PARTS = 16384
 HOPS = (
     (1, 0),
     (7, 0),
@@ -76,33 +80,51 @@
     return jnp.concatenate(bytes_, axis=0)
 
 
-def pool(ids_ref, table_ref, pooled_ref):
+def pool(ids_ref, table_ref, packed_ref, pooled_ref):
     samples = ids_ref.shape[1]
     active = table_ref.shape[0]
     lanes = 128
     fields = active // lanes
     places = lax.broadcasted_iota(jnp.int32, (lanes // 4, lanes), 0)
-
-    def finish(packed, index):
-        turned = packed.T
-        counts = jnp.concatenate(
+    chunks = samples // lanes
+
+    def count(index, carry):
+        packed_ref[index] = tally(ids_ref, pl.multiple_of(index * lanes, lanes), places)
+        return carry
+
+    lax.fori_loop(0, chunks, count, 0, unroll=UNROLL)
+
+    def spread(words):
+        turned = words.T
+        return jnp.concatenate(
             [
                 ((turned >> (8 * field)) & 255).astype(jnp.float32).astype(jnp.bfloat16)
                 for field in range(fields)
             ],
             axis=1,
         )
-        pooled_ref[pl.ds(pl.multiple_of(index * lanes, lanes), lanes), :] = jnp.dot(
+
+    def look_up(index, carry):
+        counts = jnp.concatenate(
+            [spread(packed_ref[index * BATCH + part]) for part in range(BATCH)], axis=0
+        )
+        start = pl.multiple_of(index * BATCH * lanes, BATCH * lanes)
+        pooled_ref[pl.ds(start, BATCH * lanes), :] = jnp.dot(
             counts, table_ref[...], preferred_element_type=jnp.float32
         )
-
-    def chunk(index, packed):
-        finish(packed, index - 1)
-        return tally(ids_ref, pl.multiple_of(index * lanes, lanes), places)
-
-    chunks = samples // lanes
-    last = lax.fori_loop(1, chunks, chunk, tally(ids_ref, 0, places))
-    finish(last, chunks - 1)
+        return carry
+
+    lax.fori_loop(0, chunks // BATCH, look_up, 0)
+
+
+def decode(exponent, fraction):
+    return jnp.exp2(exponent.astype(jnp.float32)) * (fraction.astype(jnp.float32) / PARTS)
+
+
+def encode(top):
+    exponent = jnp.floor(jnp.log2(jnp.maximum(top, 1e-30))) + 1.0
+    fraction = (top * jnp.exp2(-exponent) * PARTS).astype(jnp.int32) + 1
+    return exponent.astype(jnp.int32), fraction
 
 
 def kernel(
@@ -116,6 +138,7 @@
     out_ref,
     ids_v,
     table_v,
+    packed,
     pooled,
     permuted,
     xsend,
@@ -125,8 +148,6 @@
     cross,
     relay,
     final,
-    relay_top,
-    final_top,
     outsum,
     second_v,
     outbox,
@@ -356,12 +377,17 @@
     pl.when(gate)(gate_towers)
     loads[0].wait()
     loads[1].wait()
-    pool(ids_v, table_v, pooled)
-    permute_send(0)
-    for n in range(RELAYED):
+    pool(ids_v, table_v, packed, pooled)
+    def relay_rows(n):
         for half, near_step in ((0, 3), (1, 1)):
             arrived_w(n, near_step).wait_recv()
             forward(n, half).start()
+
+    for n in range(AHEAD):
+        relay_rows(n)
+    permute_send(0)
+    for n in range(AHEAD, RELAYED):
+        relay_rows(n)
     for n in range(EARLY, len(SPANS)):
         for step in w_steps(n):
             send_w(n, step).start()
@@ -400,18 +426,15 @@
             device_id_type=MESH,
         )
 
-    def final_copies(g):
-        return [
-            pltpu.make_async_remote_copy(
-                src_ref=source.at[pl.ds(*GROUPS[g])],
-                dst_ref=target.at[pl.ds(*GROUPS[g])],
-                send_sem=f_send.at[g, which],
-                recv_sem=f_recv.at[g, which],
-                device_id=across,
-                device_id_type=MESH,
-            )
-            for which, (source, target) in enumerate(((relay_top, final_top), (relay, final)))
-        ]
+    def final_copy(g):
+        return pltpu.make_async_remote_copy(
+            src_ref=relay.at[pl.ds(*GROUPS[g])],
+            dst_ref=final.at[pl.ds(*GROUPS[g])],
+            send_sem=f_send.at[g],
+            recv_sem=f_recv.at[g],
+            device_id=across,
+            device_id_type=MESH,
+        )
 
     def tiles(g):
         return range(GROUPS[g][0], sum(GROUPS[g]))
@@ -436,20 +459,22 @@
         cross_copy(0, g).wait_recv()
         for n in tiles(g):
             part = total[0, n, core] + cross[0, n]
-            top = jnp.max(jnp.abs(part), axis=0, keepdims=True)
-            steps_up = part * (LEVELS / jnp.maximum(top, 1e-30)) + (LEVELS + 1.5)
-            relay[n] = (steps_up.astype(jnp.int32) - (LEVELS + 1)).astype(jnp.int16)
-            relay_top[n] = jnp.broadcast_to(top, relay_top.shape[1:])
-        for copy in final_copies(g):
-            copy.start()
+            exponent, fraction = encode(jnp.max(jnp.abs(part), axis=0, keepdims=True))
+            steps_up = part * (LEVELS / decode(exponent, fraction)) + (LEVELS + 1.5)
+            relay[n, :block, :] = (steps_up.astype(jnp.int32) - (LEVELS + 1)).astype(jnp.int16)
+            line = lax.broadcasted_iota(jnp.int32, (16, tile), 0)
+            code = jnp.where(line == 0, exponent, jnp.where(line == 1, fraction, 0))
+            relay[n, block:, :] = code.astype(jnp.int16)
+        final_copy(g).start()
 
     def second_layer(g):
         cross_copy(1, g).wait_recv()
-        for copy in final_copies(g):
-            copy.wait_recv()
+        final_copy(g).wait_recv()
         hidden = []
         for n in tiles(g):
-            other = final[n].astype(jnp.float32) * (final_top[n, 0:1, :] * (1.0 / LEVELS))
+            code = final[n, block:, :].astype(jnp.int32)
+            unit = decode(code[0:1], code[1:2]) * (1.0 / LEVELS)
+            other = final[n, :block, :].astype(jnp.float32) * unit
             preact = total[1, n, core] + cross[1, n] + other
             hidden.append(jnp.maximum(preact, 0.0).astype(jnp.bfloat16))
         begin, count = GROUPS[g]
@@ -555,8 +580,7 @@
     for g in range(groups):
         cross_copy(0, g).wait_send()
         cross_copy(1, g).wait_send()
-        for copy in final_copies(g):
-            copy.wait_send()
+        final_copy(g).wait_send()
     for dz, dx in HOPS:
         send_o(dz, dx).wait_send()
 
@@ -593,6 +617,7 @@
         scratch_shapes=[
             vmem((bag, samples), jnp.int32),
             vmem((active, emb), jnp.bfloat16),
+            vmem((samples // 128, 128, 128), jnp.int32),
             vmem((samples, emb), jnp.float32),
             vmem((block, emb), jnp.float32),
             vmem((2, RING, quarter // 2, emb), jnp.bfloat16),
@@ -600,10 +625,8 @@
             vmem((CHUNKS, RING * emb, tile), jnp.bfloat16),
             vmem((2, CHUNKS, CORES, block, tile), jnp.float32),
             vmem((2, CHUNKS, block, tile), jnp.float32),
-            vmem((CHUNKS, block, tile), jnp.int16),
-            vmem((CHUNKS, block, tile), jnp.int16),
-            vmem((CHUNKS, 8, tile), jnp.float32),
-            vmem((CHUNKS, 8, tile), jnp.float32),
+            vmem((CHUNKS, block + 16, tile), jnp.int16),
+            vmem((CHUNKS, block + 16, tile), jnp.int16),
             vmem((block, zwidth), jnp.float32),
             vmem((hidden, zwidth), jnp.bfloat16),
             vmem((towers, share, zwidth), jnp.bfloat16),
@@ -622,8 +645,8 @@
             dma((2, RING)),
             dma((2, CHUNKS)),
             dma((2, CHUNKS)),
-            dma((CHUNKS, 2)),
-            dma((CHUNKS, 2)),
+            dma((CHUNKS,)),
+            dma((CHUNKS,)),
             dma((towers,)),
             dma((towers,)),
             pltpu.SemaphoreType.REGULAR,

time: 41.8 us -> 39.6 us (0.947)
  Pallas kernels: 40.8 us -> 38.8 us
    pallas_call x1, Pallas kernels: 40.8 us -> 38.8 us  [on_device(): pl.pallas_call(functools.partial(kernel, towers=towers), out_shape=jax.Sh...]
where the time goes in v7:
time: 39.6 us; the launch traced here: 39.4 us
  Pallas kernels  38.8 us (98%)
  local copies, waits for them, and re-layouts  0.6 us (2%)
    pallas_call x1, Pallas kernels, on_device(): pl.pallas_call(functools.partial(kernel, towers=towers), out_shape=jax.Sh...  38.8 us

profile of v7, /device:TPU:1, one launch (start us, length us, event | category | flops | bytes accessed | tf_op | source)
XLA Modules:
  0.0 39.4 jit_solution(2955368809680537654)
XLA Ops:
  0.0 38.8 %shard_map.73 = f32[8,128]{1,0:T(8,128)S(1)} custom-call(s32[32,2048]{1,0:T(8,128)} %bitcast.11, bf16[512,128]{1,0:T(8,128)(2,1)} %bitcast.13, s32[2048]{0:T(1024)} %order_ref.1, bf16[128,1024]{1,0:T(8,128)(2,1)} %bitcast.12, bf16[1024,512]{1,0:T(8,128)(2,1)} %bitcast.10, bf16[16,512,128]{2,1,0:T(8,128)(2,1)} %bitcast.9, f32[256,128]{1,0:T(8,128)} %inter_hbm.1), custom_call_target="tpu_custom_call" | custom-call | tf_op jit(solution)/shard_map/pallas_call | solution.py:604
  38.9 0.6 %copy.9 = f32[1,8,128]{2,1,0:T(8,128)} copy(f32[1,8,128]{2,1,0:T(8,128)S(1)} %bitcast.8) | data formatting | bytes 8192

commit v8 on v7

--- a/solution.py
+++ b/solution.py
@@ -14,11 +14,12 @@
 CHUNKS = 8
 BATCH = 8
 UNROLL = 1
-SPANS = ((0, 4), (4, 2), (6, 2))
-GROUPS = ((0, 2), (2, 2), (4, 2), (6, 2))
+SPANS = ((0, 3), (3, 3), (6, 2))
+GROUPS = ((0, 3), (3, 3), (6, 2))
 EARLY = 2
 RELAYED = 2
 AHEAD = 0
+GATE = 1
 LEVELS = 32752
 PARTS = 16384
 HOPS = (
@@ -212,23 +213,22 @@
     loads[1].start()
     for copy in firsts:
         copy.start()
-    for copy in loads[2:]:
-        copy.start()
 
     barrier = pltpu.get_barrier_semaphore()
     devices = CORES * RING * 2
-    gate = dev == 0
+    gate = dev == GATE
     peers = [at_row(along(step))["dev"] for step in range(1, RING)]
     peers += [partner["dev"], across["dev"]]
     near = jnp.int32(0)
+    others = [other for other in range(devices) if other != GATE]
     for peer in peers:
-        near = near + jnp.where(peer == 0, 1, 0)
+        near = near + jnp.where(peer == GATE, 1, 0)
 
     @pl.when(jnp.logical_not(gate))
     def _():
         for peer in peers:
 
-            @pl.when(peer != 0)
+            @pl.when(peer != GATE)
             def _():
                 pl.semaphore_signal(
                     barrier, inc=1, device_id={"dev": peer}, device_id_type=MESH
@@ -238,15 +238,15 @@
 
         @pl.when(near == 1)
         def _():
-            pl.semaphore_signal(near_sem, inc=1, device_id={"dev": 0}, device_id_type=MESH)
+            pl.semaphore_signal(near_sem, inc=1, device_id={"dev": GATE}, device_id_type=MESH)
 
         @pl.when(near == 0)
         def _():
-            pl.semaphore_signal(far_sem, inc=1, device_id={"dev": 0}, device_id_type=MESH)
+            pl.semaphore_signal(far_sem, inc=1, device_id={"dev": GATE}, device_id_type=MESH)
 
     @pl.when(gate)
     def _():
-        for other in range(1, devices):
+        for other in others:
             pl.semaphore_signal(barrier, inc=1, device_id={"dev": other}, device_id_type=MESH)
         pl.semaphore_wait(near_sem, len(peers))
 
@@ -262,13 +262,13 @@
 
     def gate_open():
         pl.semaphore_wait(barrier, towers - 1)
-        for other in range(1, devices):
+        for other in others:
             pl.semaphore_signal(open_sem, inc=1, device_id={"dev": other}, device_id_type=MESH)
 
     for copy in firsts:
         copy.wait()
 
-    steps = (1, 3, 2)
+    steps = (3, 1, 2)
 
     def send_w(n, step):
         return pltpu.make_async_remote_copy(
@@ -319,10 +319,20 @@
             device_id_type=MESH,
         )
 
+    def half_of(kind):
+        part = 1 - core if kind == 1 else core
+        return pl.ds(pl.multiple_of(part * block, block), block)
+
+    def x_slots(kind, place, span):
+        if kind == 0:
+            return xsend.at[0, place], xall.at[0, :, span]
+        return xsend.at[1, place, half_of(kind), :], xall.at[1, half_of(kind), span]
+
     def send_x(kind, step):
-        return pltpu.make_async_remote_copy(
-            src_ref=xsend.at[kind, along(step)],
-            dst_ref=xall.at[kind, :, mine],
+        source, target = x_slots(kind, along(step), mine)
+        return pltpu.make_async_remote_copy(
+            src_ref=source,
+            dst_ref=target,
             send_sem=x_send.at[kind, step],
             recv_sem=x_recv.at[kind, row],
             device_id=at_row(along(step)),
@@ -330,20 +340,21 @@
         )
 
     def arrived_x(kind, step):
-        source = along(step)
-        span = pl.ds(pl.multiple_of(source * emb, emb), emb)
-        return pltpu.make_async_remote_copy(
-            src_ref=xsend.at[kind, source],
-            dst_ref=xall.at[kind, :, span],
+        place = along(step)
+        span = pl.ds(pl.multiple_of(place * emb, emb), emb)
+        source, target = x_slots(kind, place, span)
+        return pltpu.make_async_remote_copy(
+            src_ref=source,
+            dst_ref=target,
             send_sem=x_send.at[kind, step],
-            recv_sem=x_recv.at[kind, source],
+            recv_sem=x_recv.at[kind, place],
             device_id=partner,
             device_id_type=MESH,
         )
 
     def permute_rows(kind, place, store):
         x = 1 - col if kind == 0 else col
-        for c in range(CORES):
+        for c in ((0, 1), (1 - core,), (core,))[kind]:
             start = ((x * RING + place) * CORES + c) * block
 
             def group(index, carry):
@@ -353,21 +364,22 @@
                 return carry
 
             lax.fori_loop(0, block // 16, group, 0)
-            store(c, permuted[...].astype(jnp.bfloat16))
+            part = pl.ds(c * block, block) if kind == 0 else half_of(kind)
+            store(part, permuted[...].astype(jnp.bfloat16))
 
     def permute_send(kind):
         for step in steps:
             place = along(step)
 
             def keep(part, value):
-                xsend[kind, place, part * block : (part + 1) * block, :] = value
+                xsend[min(kind, 1), place, part, :] = value
 
             permute_rows(kind, place, keep)
             send_x(kind, step).start()
 
     def permute_own(kind):
         def keep(part, value):
-            xall[kind, part * block : (part + 1) * block, mine] = value
+            xall[min(kind, 1), part, mine] = value
 
         permute_rows(kind, row, keep)
 
@@ -378,6 +390,8 @@
     loads[0].wait()
     loads[1].wait()
     pool(ids_v, table_v, packed, pooled)
+    for copy in loads[2:]:
+        copy.start()
     def relay_rows(n):
         for half, near_step in ((0, 3), (1, 1)):
             arrived_w(n, near_step).wait_recv()
@@ -393,7 +407,9 @@
             send_w(n, step).start()
     permute_own(0)
     permute_send(1)
+    permute_send(2)
     permute_own(1)
+    permute_own(2)
     pl.when(gate)(gate_open)
 
     loads[4].wait()
@@ -451,9 +467,15 @@
 
     def first_layer(kind, g):
         for n in tiles(g):
-            part = jnp.dot(xall[kind], wall[n], preferred_element_type=jnp.float32)
-            total[kind, n] = part.reshape(CORES, block, tile)
-        cross_copy(kind, g).start()
+            if kind == 0:
+                part = jnp.dot(xall[0], wall[n], preferred_element_type=jnp.float32)
+                total[0, n] = part.reshape(CORES, block, tile)
+            else:
+                total[1, n, 1 - core if kind == 1 else core] = jnp.dot(
+                    xall[1, half_of(kind), :], wall[n], preferred_element_type=jnp.float32
+                )
+        if kind < 2:
+            cross_copy(kind, g).start()
 
     def add_cores(g):
         cross_copy(0, g).wait_recv()
@@ -501,6 +523,10 @@
         arrived_x(1, step).wait_recv()
     for g in range(groups):
         first_layer(1, g)
+    for step in steps:
+        arrived_x(2, step).wait_recv()
+    for g in range(groups):
+        first_layer(2, g)
     for g in range(groups):
         second_layer(g)
 
@@ -571,6 +597,7 @@
     for step in steps:
         send_x(0, step).wait_send()
         send_x(1, step).wait_send()
+        send_x(2, step).wait_send()
         for n in range(len(SPANS)):
             if step in w_steps(n):
                 send_w(n, step).wait_send()
@@ -641,8 +668,8 @@
             dma((len(SPANS), RING)),
             dma((len(SPANS), 2)),
             dma((len(SPANS), 2)),
-            dma((2, RING)),
-            dma((2, RING)),
+            dma((3, RING)),
+            dma((3, RING)),
             dma((2, CHUNKS)),
             dma((2, CHUNKS)),
             dma((CHUNKS,)),

time: 39.6 us -> 38.6 us (0.975)
  Pallas kernels: 38.8 us -> 37.7 us
    pallas_call x1, Pallas kernels: 38.8 us -> 37.7 us  [on_device(): pl.pallas_call(functools.partial(kernel, towers=towers), out_shape=jax.Sh...]
where the time goes in v8:
time: 38.6 us; the launch traced here: 38.3 us
  Pallas kernels  37.7 us (98%)
  local copies, waits for them, and re-layouts  0.6 us (2%)
    pallas_call x1, Pallas kernels, on_device(): pl.pallas_call(functools.partial(kernel, towers=towers), out_shape=jax.Sh...  37.7 us

profile of v8, /device:TPU:1, one launch (start us, length us, event | category | flops | bytes accessed | tf_op | source)
XLA Modules:
  0.0 38.3 jit_solution(14622399485420514505)
XLA Ops:
  0.0 37.7 %shard_map.73 = f32[8,128]{1,0:T(8,128)S(1)} custom-call(s32[32,2048]{1,0:T(8,128)} %bitcast.11, bf16[512,128]{1,0:T(8,128)(2,1)} %bitcast.13, s32[2048]{0:T(1024)} %order_ref.1, bf16[128,1024]{1,0:T(8,128)(2,1)} %bitcast.12, bf16[1024,512]{1,0:T(8,128)(2,1)} %bitcast.10, bf16[16,512,128]{2,1,0:T(8,128)(2,1)} %bitcast.9, f32[256,128]{1,0:T(8,128)} %inter_hbm.1), custom_call_target="tpu_custom_call" | custom-call | tf_op jit(solution)/shard_map/pallas_call | solution.py:631
  37.7 0.6 %copy.9 = f32[1,8,128]{2,1,0:T(8,128)} copy(f32[1,8,128]{2,1,0:T(8,128)S(1)} %bitcast.8) | data formatting | bytes 8192

commit v9 on v8

--- a/solution.py
+++ b/solution.py
@@ -513,12 +513,10 @@
     groups = len(GROUPS)
     for step in steps:
         arrived_x(0, step).wait_recv()
-    for g in range(groups + 1):
-        if g < groups:
-            arrived_span(g)
-            first_layer(0, g)
-        if g >= 1:
-            add_cores(g - 1)
+    for g in range(groups):
+        arrived_span(g)
+        first_layer(0, g)
+        add_cores(g)
     for step in steps:
         arrived_x(1, step).wait_recv()
     for g in range(groups):

time: 38.6 us -> 38.9 us (level)
  no operation moved by 1% of the time
where the time goes in v9:
time: 38.9 us; the launch traced here: 38.2 us
  Pallas kernels  37.6 us (97%)
  local copies, waits for them, and re-layouts  0.6 us (2%)
    pallas_call x1, Pallas kernels, on_device(): pl.pallas_call(functools.partial(kernel, towers=towers), out_shape=jax.Sh...  37.6 us

profile of v9, /device:TPU:1, one launch (start us, length us, event | category | flops | bytes accessed | tf_op | source)
XLA Modules:
  0.0 38.2 jit_solution(14704609549396470633)
XLA Ops:
  0.0 37.6 %shard_map.73 = f32[8,128]{1,0:T(8,128)S(1)} custom-call(s32[32,2048]{1,0:T(8,128)} %bitcast.11, bf16[512,128]{1,0:T(8,128)(2,1)} %bitcast.13, s32[2048]{0:T(1024)} %order_ref.1, bf16[128,1024]{1,0:T(8,128)(2,1)} %bitcast.12, bf16[1024,512]{1,0:T(8,128)(2,1)} %bitcast.10, bf16[16,512,128]{2,1,0:T(8,128)(2,1)} %bitcast.9, f32[256,128]{1,0:T(8,128)} %inter_hbm.1), custom_call_target="tpu_custom_call" | custom-call | tf_op jit(solution)/shard_map/pallas_call | solution.py:629
  37.6 0.6 %copy.9 = f32[1,8,128]{2,1,0:T(8,128)} copy(f32[1,8,128]{2,1,0:T(8,128)S(1)} %bitcast.8) | data formatting | bytes 8192

commit v10 on v8

--- a/solution.py
+++ b/solution.py
@@ -15,7 +15,7 @@
 BATCH = 8
 UNROLL = 1
 SPANS = ((0, 3), (3, 3), (6, 2))
-GROUPS = ((0, 3), (3, 3), (6, 2))
+GROUPS = ((0, 3), (3, 3), (6, 1), (7, 1))
 EARLY = 2
 RELAYED = 2
 AHEAD = 0

time: 38.6 us -> 38.8 us (level)
  no operation moved by 1% of the time
where the time goes in v10:
time: 38.8 us; the launch traced here: 38.3 us
  Pallas kernels  37.7 us (97%)
  local copies, waits for them, and re-layouts  0.6 us (2%)
    pallas_call x1, Pallas kernels, on_device(): pl.pallas_call(functools.partial(kernel, towers=towers), out_shape=jax.Sh...  37.7 us

profile of v10, /device:TPU:1, one launch (start us, length us, event | category | flops | bytes accessed | tf_op | source)
XLA Modules:
  0.0 38.3 jit_solution(6532857423927266377)
XLA Ops:
  0.0 37.7 %shard_map.73 = f32[8,128]{1,0:T(8,128)S(1)} custom-call(s32[32,2048]{1,0:T(8,128)} %bitcast.11, bf16[512,128]{1,0:T(8,128)(2,1)} %bitcast.13, s32[2048]{0:T(1024)} %order_ref.1, bf16[128,1024]{1,0:T(8,128)(2,1)} %bitcast.12, bf16[1024,512]{1,0:T(8,128)(2,1)} %bitcast.10, bf16[16,512,128]{2,1,0:T(8,128)(2,1)} %bitcast.9, f32[256,128]{1,0:T(8,128)} %inter_hbm.1), custom_call_target="tpu_custom_call" | custom-call | tf_op jit(solution)/shard_map/pallas_call | solution.py:631
  37.7 0.6 %copy.9 = f32[1,8,128]{2,1,0:T(8,128)} copy(f32[1,8,128]{2,1,0:T(8,128)S(1)} %bitcast.8) | data formatting | bytes 8192
